TPU v7x, 32 devices: a whole 2x2x4 slice. The times are simulated.
32 devices in a mesh: dp: 4 (over x, y), tp: 8 (over z, core).
Axes of the slice: x: 2, y: 2, z: 4, core: 2. Of those that a mesh axis runs over, the one named last changes fastest.
Arguments:
- x: bfloat16 [512, 5120], P('dp'), parts along dimension 0
- w_gate: bfloat16 [5120, 12288], P(None, 'tp')
- w_up: bfloat16 [5120, 12288], P(None, 'tp')
- w_down: bfloat16 [12288, 5120], P('tp')
Outputs:
- output: bfloat16 [512, 5120], P('dp'), parts along dimension 0
There are 4 independent parts. A program takes and returns all parts, laid end to end along the dimension named above; an argument that names none is the same for every part.
All inputs are finite; a program needn't handle non-finite values.
Results may differ from a plain program's by a relative error of at most 0.016.
Values are sent between devices in bfloat16 or wider.
A program may use at most 2 GiB of HBM per device.

v0:
```python
import jax
import jax.numpy as jnp
from jax import lax
from jax.sharding import PartitionSpec as P


def solution(mesh):
    def step(x, w_gate, w_up, w_down):
        gate = jnp.dot(x, w_gate, preferred_element_type=jnp.float32)
        up = jnp.dot(x, w_up, preferred_element_type=jnp.float32)
        hidden = (jax.nn.silu(gate) * up).astype(jnp.bfloat16)
        term = jnp.dot(hidden, w_down, preferred_element_type=jnp.float32).astype(jnp.bfloat16)
        return lax.psum(term, "tp")

    return jax.shard_map(
        step,
        mesh=mesh,
        in_specs=(P("dp", None), P(None, "tp"), P(None, "tp"), P("tp", None)),
        out_specs=P("dp", None),
        check_vma=False,
    )
```

profile of v0, /device:TPU:0, one launch (start us, length us, event | category | flops | bytes accessed | tf_op | source)
XLA Modules:
  0.0 103.4 jit_solution(16925731400302566906)
XLA Ops:
  6.5 0.0 copy-start
  6.5 0.0 all-reduce.2.cloned.1.call-start
  6.5 1.3 %copy-done = bf16[128,5120]{1,0:T(8,128)(2,1)S(1)} copy-done((bf16[128,5120]{1,0:T(8,128)(2,1)S(1)}, bf16[128,5120]{1,0:T(8,128)(2,1)}, u32[]{:S(2)}) %copy-start) | copy-done | bytes 1310744
  7.9 7.7 %fusion.3 = f32[128,1536]{1,0:T(8,128)S(1)} fusion(bf16[128,5120]{1,0:T(8,128)(2,1)S(1)} %copy-done, bf16[5120,1536]{1,0:T(8,128)(2,1)} %param.5), kind=kOutput, calls=%fused_computation.5 | convolution fusion | flops 2013265920 | bytes 17825792 | tf_op jit(solution)/shard_map/dot_general | solution.py:9
  15.5 15.5 %convolution_convert_fusion = bf16[128,5120]{1,0:T(8,128)(2,1)} fusion(bf16[1536,5120]{1,0:T(8,128)(2,1)} %param.7, bf16[128,5120]{1,0:T(8,128)(2,1)S(1)} %copy-done, bf16[5120,1536]{1,0:T(8,128)(2,1)} %param.6, f32[128,1536]{1,0:T(8,128)S(1)} %fusion.3), kind=kOutput, calls=%fused_computation | convolution fusion | flops 4028366848 | bytes 34865152 | tf_op jit(solution)/shard_map/dot_general | solution.py:12
  31.0 0.0 all-reduce.2.cloned.1.call-update
  31.0 63.1 %all-reduce.2.cloned.1.call-done = bf16[128,5120]{1,0:T(8,128)(2,1)} async-done(((bf16[128,5120]{1,0:T(8,128)(2,1)}), bf16[128,5120]{1,0:T(8,128)(2,1)}) %all-reduce.2.cloned.1.call-update) | async-done | bytes 1310736 | tf_op jit(solution)/shard_map/psum | solution.py:13
  94.1 2.5 %copy.6 = bf16[128,5120]{1,0:T(8,128)(2,1)} copy(bf16[128,5120]{1,0:T(8,128)(2,1)} %all-reduce.2.cloned.1.call-done) | data formatting | bytes 2621440
Async XLA Ops:
  6.5 1.3 %copy-start = (bf16[128,5120]{1,0:T(8,128)(2,1)S(1)}, bf16[128,5120]{1,0:T(8,128)(2,1)}, u32[]{:S(2)}) copy-start(bf16[128,5120]{1,0:T(8,128)(2,1)} %param.4) | copy-start | bytes 3932164
  6.5 87.6 %all-reduce.2.cloned.1.call-start = ((), (), s32[]{:S(2)}) async-start(), calls=%async_computation | async-start | bytes 2621440 | tf_op jit(solution)/shard_map/psum | solution.py:13
Sparse Core Ops, SparseCore 0:
  31.2 62.9 all-reduce.1
where the time goes:
time: 104 us; the launch traced here: 103 us
  waiting for transfers between devices  63.1 us (61%)
  matrix products  23.2 us (22%)
  between operations  13.4 us (13%)
  local copies, waits for them, and re-layouts  3.77 us (4%)
    psum x1, waiting for transfers between devices, step(): return lax.psum(term, 'tp')  63.1 us
    dot_general x1, matrix products, step(): jnp.dot(hidden, w_down, preferred_element_type=jnp.float32)  15.5 us
    dot_general x1, matrix products, step(): gate = jnp.dot(x, w_gate, preferred_element_type=jnp.float32)  7.67 us
    unnamed x3, local copies, waits for them, and re-layouts  3.77 us
  transfers between devices with their start and end apart: 1, of which 1 were waited for; matrix products, arithmetic and copies ran while one was open for 0% of the time, Pallas kernels for 0%

commit v1 on v0

v1 whole, which is shorter than its diff:
```python
import functools

import jax
import jax.numpy as jnp
from jax import lax
from jax.experimental import pallas as pl
from jax.experimental.pallas import tpu as pltpu
from jax.sharding import PartitionSpec as P

MESH = pl.DeviceIdType.MESH
F32, BF16 = jnp.float32, jnp.bfloat16

GU_COLS = 256
GU_PARTS = 4
Y_COLS = 256
D2D_LAG = 4
IN_START = 14
FIN_LAG = 4


def kernel(
    x_hbm, wg_hbm, wu_hbm, wd_hbm, y_ref,
    x_v, wg_v, wu_v, wd_v, g_acc, u_acc, hid, own, snd, rcv, part, a_rcv, b_rcv,
    x_sem, wg_sem, wu_sem, wd_sem,
    d_ss, d_rs, p_ss, p_rs, f_ss, f_rs, g_ss, g_rs,
):
    tp = lax.axis_index("tp")
    core = lax.rem(tp, 2)
    z = lax.div(tp, 2)
    sibling = tp + 1 - 2 * core
    inner = jnp.logical_and(z > 0, z < 3)
    outer = jnp.logical_not(inner)
    low = z < 2
    onward = jnp.where(low, tp + 2, tp - 2)
    back = jnp.where(low, tp - 2, tp + 2)

    rows, half = x_v.shape[0], x_v.shape[0] // 2
    kd = wg_v.shape[1]
    n_j = wg_v.shape[0] // GU_PARTS
    n_k = wd_v.shape[0]
    mine = pl.ds(pl.multiple_of(core * half, half), half)
    theirs = pl.ds(pl.multiple_of((1 - core) * half, half), half)

    barrier = pltpu.get_barrier_semaphore()
    pl.semaphore_signal(barrier, inc=1, device_id={"tp": sibling}, device_id_type=MESH)
    pl.semaphore_signal(barrier, inc=1, device_id={"tp": onward}, device_id_type=MESH)

    @pl.when(inner)
    def _():
        pl.semaphore_signal(barrier, inc=1, device_id={"tp": back}, device_id_type=MESH)

    def ycols(k):
        return pl.ds(pl.multiple_of(k * Y_COLS, Y_COLS), Y_COLS)

    def x_copy(part_rows, i):
        return pltpu.make_async_copy(
            x_hbm.at[part_rows, :], x_v.at[pl.ds(i * half, half), :], x_sem.at[i]
        )

    def gu_copy(hbm, vmem, sem, j, p):
        i = j * GU_PARTS + p
        return pltpu.make_async_copy(
            hbm.at[
                pl.ds(pl.multiple_of(p * kd, kd), kd),
                pl.ds(pl.multiple_of(j * GU_COLS, GU_COLS), GU_COLS),
            ],
            vmem.at[i],
            sem.at[i],
        )

    def wd_copy(k):
        return pltpu.make_async_copy(wd_hbm.at[:, ycols(k)], wd_v.at[k], wd_sem.at[k])

    x_copy(mine, 0).start()
    x_copy(theirs, 1).start()

    def start_gu(j, c):
        for p in range(GU_PARTS):
            gu_copy(wg_hbm, wg_v, wg_sem, j, p).start()
            gu_copy(wu_hbm, wu_v, wu_sem, j, p).start()
        return c

    lax.fori_loop(0, n_j, start_gu, 0)

    def start_wd(k, c):
        wd_copy(k).start()
        return c

    lax.fori_loop(0, n_k, start_wd, 0)

    x_copy(mine, 0).wait()
    x_copy(theirs, 1).wait()

    def gate_up(j, c):
        for p in range(GU_PARTS):
            i = j * GU_PARTS + p
            xs = x_v[:, p * kd : (p + 1) * kd]
            gu_copy(wg_hbm, wg_v, wg_sem, j, p).wait()
            gu_copy(wu_hbm, wu_v, wu_sem, j, p).wait()
            g = jnp.dot(xs, wg_v[i], preferred_element_type=F32)
            u = jnp.dot(xs, wu_v[i], preferred_element_type=F32)
            if p == 0:
                g_acc[...] = g
                u_acc[...] = u
            elif p < GU_PARTS - 1:
                g_acc[...] += g
                u_acc[...] += u
            else:
                g = g_acc[...] + g
                u = u_acc[...] + u
                hid[:, pl.ds(pl.multiple_of(j * GU_COLS, GU_COLS), GU_COLS)] = (
                    jax.nn.silu(g) * u
                ).astype(BF16)
        return c

    lax.fori_loop(0, n_j, gate_up, 0)

    def d2d(k):
        return pltpu.make_async_remote_copy(
            src_ref=snd.at[k], dst_ref=rcv.at[k], send_sem=d_ss.at[k], recv_sem=d_rs.at[k],
            device_id={"tp": sibling}, device_id_type=MESH,
        )

    def to_inner(k):
        return pltpu.make_async_remote_copy(
            src_ref=part.at[k], dst_ref=a_rcv.at[k], send_sem=p_ss.at[k], recv_sem=p_rs.at[0, k],
            device_id={"tp": onward}, device_id_type=MESH,
        )

    def across(k):
        return pltpu.make_async_remote_copy(
            src_ref=part.at[k], dst_ref=b_rcv.at[k], send_sem=p_ss.at[k], recv_sem=p_rs.at[1, k],
            device_id={"tp": onward}, device_id_type=MESH,
        )

    def to_outer(k):
        return pltpu.make_async_remote_copy(
            src_ref=y_ref.at[mine, ycols(k)], dst_ref=y_ref.at[mine, ycols(k)],
            send_sem=f_ss.at[k], recv_sem=f_rs.at[k],
            device_id={"tp": back}, device_id_type=MESH,
        )

    def share(k):
        return pltpu.make_async_remote_copy(
            src_ref=y_ref.at[mine, ycols(k)], dst_ref=y_ref.at[mine, ycols(k)],
            send_sem=g_ss.at[k], recv_sem=g_rs.at[k],
            device_id={"tp": sibling}, device_id_type=MESH,
        )

    def share_arrival(k):
        return pltpu.make_async_remote_copy(
            src_ref=y_ref.at[theirs, ycols(k)], dst_ref=y_ref.at[theirs, ycols(k)],
            send_sem=g_ss.at[k], recv_sem=g_rs.at[k],
            device_id={"tp": sibling}, device_id_type=MESH,
        )

    def term(k):
        wd_copy(k).wait()
        t = jnp.dot(hid[...], wd_v[k], preferred_element_type=F32)
        own[k] = t[:half]
        snd[k] = t[half:].astype(BF16)
        d2d(k).start()

    def outer_sum(k):
        d2d(k).wait_recv()
        part[k] = (own[k] + rcv[k].astype(F32)).astype(BF16)
        to_inner(k).start()

    def inner_sum(k):
        d2d(k).wait_recv()
        to_inner(k).wait_recv()
        part[k] = (own[k] + rcv[k].astype(F32) + a_rcv[k].astype(F32)).astype(BF16)
        across(k).start()

    def inner_final(k):
        across(k).wait_recv()
        y_ref[mine, ycols(k)] = (part[k].astype(F32) + b_rcv[k].astype(F32)).astype(BF16)
        to_outer(k).start()
        share(k).start()

    def outer_final(k):
        to_outer(k).wait_recv()
        share(k).start()

    @pl.when(inner)
    def _():
        pl.semaphore_wait(barrier, 3)

    @pl.when(outer)
    def _():
        pl.semaphore_wait(barrier, 2)

    def terms(k, c):
        term(k)

        @pl.when(jnp.logical_and(outer, k >= D2D_LAG))
        def _():
            outer_sum(k - D2D_LAG)

        @pl.when(jnp.logical_and(inner, k >= IN_START))
        def _():
            inner_sum(k - IN_START)

        return c

    lax.fori_loop(0, n_k, terms, 0)

    def loop(lo, hi, f):
        def it(k, c):
            f(k)
            return c

        lax.fori_loop(lo, hi, it, 0)

    @pl.when(outer)
    def _():
        loop(n_k - D2D_LAG, n_k, outer_sum)
        loop(0, n_k, outer_final)
        loop(0, n_k, lambda k: to_inner(k).wait_send())

    @pl.when(inner)
    def _():
        first = n_k - IN_START
        loop(0, first - FIN_LAG, inner_final)

        def both(k):
            inner_sum(k)
            inner_final(k - FIN_LAG)

        loop(max(first, FIN_LAG), n_k, both)
        loop(n_k - FIN_LAG, n_k, inner_final)

        def sent(k):
            across(k).wait_send()
            to_outer(k).wait_send()

        loop(0, n_k, sent)

    def finish(k):
        d2d(k).wait_send()
        share(k).wait_send()
        share_arrival(k).wait_recv()

    loop(0, n_k, finish)


def solution(mesh):
    def step(x, w_gate, w_up, w_down):
        rows, depth = x.shape
        width = w_gate.shape[1]
        out = w_down.shape[1]
        half = rows // 2
        n_gu = (width // GU_COLS) * GU_PARTS
        n_k = out // Y_COLS
        kd = depth // GU_PARTS
        dma = pltpu.SemaphoreType.DMA
        return pl.pallas_call(
            kernel,
            out_shape=jax.ShapeDtypeStruct((rows, out), BF16),
            in_specs=[pl.BlockSpec(memory_space=pl.ANY)] * 4,
            out_specs=pl.BlockSpec(memory_space=pltpu.VMEM),
            scratch_shapes=[
                pltpu.VMEM((rows, depth), BF16),
                pltpu.VMEM((n_gu, kd, GU_COLS), BF16),
                pltpu.VMEM((n_gu, kd, GU_COLS), BF16),
                pltpu.VMEM((n_k, width, Y_COLS), BF16),
                pltpu.VMEM((rows, GU_COLS), F32),
                pltpu.VMEM((rows, GU_COLS), F32),
                pltpu.VMEM((rows, width), BF16),
                pltpu.VMEM((n_k, half, Y_COLS), F32),
                pltpu.VMEM((n_k, half, Y_COLS), BF16),
                pltpu.VMEM((n_k, half, Y_COLS), BF16),
                pltpu.VMEM((n_k, half, Y_COLS), BF16),
                pltpu.VMEM((n_k, half, Y_COLS), BF16),
                pltpu.VMEM((n_k, half, Y_COLS), BF16),
                dma((2,)),
                dma((n_gu,)),
                dma((n_gu,)),
                dma((n_k,)),
                dma((n_k,)),
                dma((n_k,)),
                dma((n_k,)),
                dma((2, n_k)),
                dma((n_k,)),
                dma((n_k,)),
                dma((n_k,)),
                dma((n_k,)),
            ],
            compiler_params=pltpu.CompilerParams(
                collective_id=0, has_side_effects=True, vmem_limit_bytes=62 * 1024 * 1024
            ),
        )(x, w_gate, w_up, w_down)

    return jax.shard_map(
        step,
        mesh=mesh,
        in_specs=(P("dp", None), P(None, "tp"), P(None, "tp"), P("tp", None)),
        out_specs=P("dp", None),
        check_vma=False,
    )
```

time: 104 us -> 44.4 us (0.43)
  waiting for transfers between devices: 63.1 us -> 0 us
  Pallas kernels: 0 us -> 41.8 us
  matrix products: 23.2 us -> 0 us
  between operations: 13.4 us -> 0.01 us
  local copies, waits for them, and re-layouts: 3.77 us -> 2.46 us
    psum x1 -> x0, waiting for transfers between devices: 63.1 us -> none  [step(): return lax.psum(term, 'tp')]
    pallas_call x0 -> x1, Pallas kernels: none -> 41.8 us  [step(): pl.pallas_call(kernel, out_shape=jax.ShapeDtypeStruct((rows, out), BF16),...]
    dot_general x2 -> x0, matrix products: 23.2 us -> none  [the longest x1 15.5 us: step(): jnp.dot(hidden, w_down, preferred_element_type=jnp.float32)]
    unnamed x3 -> x1, local copies, waits for them, and re-layouts: 3.77 us -> 2.46 us
  transfers between devices with their start and end apart: 1 -> 0, of which waited for: 1 -> 0; matrix products, arithmetic and copies ran while one was open for 0% -> 0% of each run, Pallas kernels for 0% -> 0%
where the time goes in v1:
time: 44.4 us; the launch traced here: 44.2 us
  Pallas kernels  41.8 us (94%)
  local copies, waits for them, and re-layouts  2.46 us (6%)
    pallas_call x1, Pallas kernels, step(): pl.pallas_call(kernel, out_shape=jax.ShapeDtypeStruct((rows, out), BF16),...  41.8 us
    unnamed x1, local copies, waits for them, and re-layouts  2.46 us

profile of v1, /device:TPU:0, one launch (start us, length us, event | category | flops | bytes accessed | tf_op | source)
XLA Modules:
  0.0 44.2 jit_solution(13005737284972813069)
XLA Ops:
  0.0 41.8 %shard_map.46 = bf16[128,5120]{1,0:T(8,128)(2,1)} custom-call(bf16[128,5120]{1,0:T(8,128)(2,1)} %x_hbm.1, bf16[5120,1536]{1,0:T(8,128)(2,1)} %wg_hbm.1, bf16[5120,1536]{1,0:T(8,128)(2,1)} %wu_hbm.1, bf16[1536,5120]{1,0:T(8,128)(2,1)} %wd_hbm.1), custom_call_target="tpu_custom_call" | custom-call | tf_op jit(solution)/shard_map/pallas_call | solution.py:257
  41.8 2.5 %copy.6 = bf16[128,5120]{1,0:T(8,128)(2,1)} copy(bf16[128,5120]{1,0:T(8,128)(2,1)} %shard_map.46) | data formatting | bytes 2621440

commit v2 on v1

--- a/solution.py
+++ b/solution.py
@@ -256,7 +256,7 @@
         dma = pltpu.SemaphoreType.DMA
         return pl.pallas_call(
             kernel,
-            out_shape=jax.ShapeDtypeStruct((rows, out), BF16),
+            out_shape=pltpu.VMEM((rows, out), BF16),
             in_specs=[pl.BlockSpec(memory_space=pl.ANY)] * 4,
             out_specs=pl.BlockSpec(memory_space=pltpu.VMEM),
             scratch_shapes=[
@@ -287,7 +287,7 @@
                 dma((n_k,)),
             ],
             compiler_params=pltpu.CompilerParams(
-                collective_id=0, has_side_effects=True, vmem_limit_bytes=62 * 1024 * 1024
+                collective_id=0, has_side_effects=True, vmem_limit_bytes=58 * 1024 * 1024
             ),
         )(x, w_gate, w_up, w_down)
 

time: 44.4 us -> 41.9 us (0.944)
  local copies, waits for them, and re-layouts: 2.46 us -> 1.06 us
  Pallas kernels: 41.8 us -> 40.7 us
    unnamed x1, local copies, waits for them, and re-layouts: 2.46 us -> 1.06 us
    pallas_call x1, Pallas kernels: 41.8 us -> 40.7 us  [step(): pl.pallas_call(kernel, out_shape=pltpu.VMEM((rows, out), BF16), in_specs=...]
where the time goes in v2:
time: 41.9 us; the launch traced here: 41.8 us
  Pallas kernels  40.7 us (97%)
  local copies, waits for them, and re-layouts  1.06 us (3%)
    pallas_call x1, Pallas kernels, step(): pl.pallas_call(kernel, out_shape=pltpu.VMEM((rows, out), BF16), in_specs=...  40.7 us
    unnamed x1, local copies, waits for them, and re-layouts  1.06 us

profile of v2, /device:TPU:0, one launch (start us, length us, event | category | flops | bytes accessed | tf_op | source)
XLA Modules:
  0.0 41.8 jit_solution(10783156498564487359)
XLA Ops:
  0.0 40.7 %shard_map.46 = bf16[128,5120]{1,0:T(8,128)(2,1)S(1)} custom-call(bf16[128,5120]{1,0:T(8,128)(2,1)} %x_hbm.1, bf16[5120,1536]{1,0:T(8,128)(2,1)} %wg_hbm.1, bf16[5120,1536]{1,0:T(8,128)(2,1)} %wu_hbm.1, bf16[1536,5120]{1,0:T(8,128)(2,1)} %wd_hbm.1), custom_call_target="tpu_custom_call" | custom-call | tf_op jit(solution)/shard_map/pallas_call | solution.py:257
  40.7 1.1 %copy.6 = bf16[128,5120]{1,0:T(8,128)(2,1)} copy(bf16[128,5120]{1,0:T(8,128)(2,1)S(1)} %shard_map.46) | data formatting | bytes 2621440

commit v3 on v2

--- a/solution.py
+++ b/solution.py
@@ -12,10 +12,10 @@
 
 GU_COLS = 256
 GU_PARTS = 4
-Y_COLS = 256
-D2D_LAG = 4
-IN_START = 14
-FIN_LAG = 4
+Y_COLS = 512
+D2D_LAG = 2
+IN_START = 8
+FIN_LAG = 2
 
 
 def kernel(

time: 41.9 us -> 42.7 us (1.019)
  Pallas kernels: 40.7 us -> 41.5 us
    pallas_call x1, Pallas kernels: 40.7 us -> 41.5 us  [step(): pl.pallas_call(kernel, out_shape=pltpu.VMEM((rows, out), BF16), in_specs=...]
where the time goes in v3:
time: 42.7 us; the launch traced here: 42.6 us
  Pallas kernels  41.5 us (97%)
  local copies, waits for them, and re-layouts  1.06 us (2%)
    pallas_call x1, Pallas kernels, step(): pl.pallas_call(kernel, out_shape=pltpu.VMEM((rows, out), BF16), in_specs=...  41.5 us
    unnamed x1, local copies, waits for them, and re-layouts  1.06 us

profile of v3, /device:TPU:0, one launch (start us, length us, event | category | flops | bytes accessed | tf_op | source)
XLA Modules:
  0.0 42.6 jit_solution(13805131197065219775)
XLA Ops:
  0.0 41.5 %shard_map.46 = bf16[128,5120]{1,0:T(8,128)(2,1)S(1)} custom-call(bf16[128,5120]{1,0:T(8,128)(2,1)} %x_hbm.1, bf16[5120,1536]{1,0:T(8,128)(2,1)} %wg_hbm.1, bf16[5120,1536]{1,0:T(8,128)(2,1)} %wu_hbm.1, bf16[1536,5120]{1,0:T(8,128)(2,1)} %wd_hbm.1), custom_call_target="tpu_custom_call" | custom-call | tf_op jit(solution)/shard_map/pallas_call | solution.py:257
  41.5 1.1 %copy.6 = bf16[128,5120]{1,0:T(8,128)(2,1)} copy(bf16[128,5120]{1,0:T(8,128)(2,1)S(1)} %shard_map.46) | data formatting | bytes 2621440

commit v4 on v0

v4 whole, which is shorter than its diff:
```python
import jax
import jax.numpy as jnp
from jax import lax
from jax.experimental import pallas as pl
from jax.experimental.pallas import tpu as pltpu
from jax.sharding import PartitionSpec as P

MESH = pl.DeviceIdType.MESH
F32, BF16 = jnp.float32, jnp.bfloat16

GU_COLS = 256
GU_PARTS = 4
UNIT = 128
PIECES = (
    (1, 1), (0, 2), (1, 2), (0, 2), (1, 3), (0, 3), (1, 4), (0, 4),
    (1, 4), (0, 4), (1, 4), (0, 2), (1, 2), (0, 1), (1, 1), (1, 1),
)
HEAD = (0,)
TAIL = (15,)
OUT_LAG = 9
IN_START, IN_RATE = 28, 3.0
HOP = 7.0


def layout():
    u, local, pieces = 0, [0, 0], []
    for owner, n in PIECES:
        pieces.append((owner, u, n, local[owner]))
        u += n
        local[owner] += n
    return pieces, u, max(local)


def kernel(
    x_hbm, wg_hbm, wu_hbm, wd_hbm, y_ref,
    x_v, wg_v, wu_v, wd_v, g_acc, u_acc, hid, own, snd, rcv, part, a_rcv, b_rcv, h_rcv,
    x_sem, wg_sem, wu_sem, wd_sem,
    d_ss, d_rs, a_ss, a_rs, b_ss, b_rs, f_ss, f_rs, g_ss, g_rs, h_ss, h_rs, t_ss,
):
    pieces, _, _ = layout()
    count = len(pieces)
    tp = lax.axis_index("tp")
    core = lax.rem(tp, 2)
    z = lax.div(tp, 2)
    sibling = tp + 1 - 2 * core
    inner = jnp.logical_and(z > 0, z < 3)
    outer = jnp.logical_not(inner)
    low = z < 2
    step = jnp.where(low, 2, -2)
    onward = tp + step
    back = tp - step
    far = tp + 2 * step

    kd = wg_v.shape[1]
    n_j = wg_v.shape[0] // GU_PARTS
    depth = x_v.shape[1]

    def signal(dev):
        pl.semaphore_signal(barrier, inc=1, device_id={"tp": dev}, device_id_type=MESH)

    barrier = pltpu.get_barrier_semaphore()
    signal(sibling)
    signal(onward)
    signal(far)
    signal(jnp.where(inner, back, onward) + 1 - 2 * core)

    @pl.when(inner)
    def _():
        signal(back)

    def cols(c):
        _, u, n, _ = pieces[c]
        return slice(u * UNIT, (u + n) * UNIT)

    def held(c):
        _, _, n, at = pieces[c]
        return slice(at, at + n)

    def made(c):
        _, u, n, _ = pieces[c]
        return slice(u, u + n)

    def gu_copy(hbm, vmem, sem, j, p):
        i = j * GU_PARTS + p
        return pltpu.make_async_copy(
            hbm.at[
                pl.ds(pl.multiple_of(p * kd, kd), kd),
                pl.ds(pl.multiple_of(j * GU_COLS, GU_COLS), GU_COLS),
            ],
            vmem.at[i],
            sem.at[i],
        )

    def wd_copy(c):
        return pltpu.make_async_copy(wd_hbm.at[:, cols(c)], wd_v.at[:, cols(c)], wd_sem.at[c])

    x_copy = pltpu.make_async_copy(x_hbm, x_v, x_sem)
    x_copy.start()

    def start_gu(j, c):
        for p in range(GU_PARTS):
            gu_copy(wg_hbm, wg_v, wg_sem, j, p).start()
            gu_copy(wu_hbm, wu_v, wu_sem, j, p).start()
        return c

    lax.fori_loop(0, n_j, start_gu, 0)
    for c in range(count):
        wd_copy(c).start()
    x_copy.wait()

    def gate_up(j, carry):
        for p in range(GU_PARTS):
            i = j * GU_PARTS + p
            xs = x_v[:, p * kd : (p + 1) * kd]
            gu_copy(wg_hbm, wg_v, wg_sem, j, p).wait()
            gu_copy(wu_hbm, wu_v, wu_sem, j, p).wait()
            g = jnp.dot(xs, wg_v[i], preferred_element_type=F32)
            u = jnp.dot(xs, wu_v[i], preferred_element_type=F32)
            if p == 0:
                g_acc[...] = g
                u_acc[...] = u
            elif p < GU_PARTS - 1:
                g_acc[...] += g
                u_acc[...] += u
            else:
                g = g_acc[...] + g
                u = u_acc[...] + u
                hid[:, pl.ds(pl.multiple_of(j * GU_COLS, GU_COLS), GU_COLS)] = (
                    jax.nn.silu(g) * u
                ).astype(BF16)
        return carry

    lax.fori_loop(0, n_j, gate_up, 0)

    def remote(src, dst, send, recv, dev):
        return pltpu.make_async_remote_copy(
            src_ref=src, dst_ref=dst, send_sem=send, recv_sem=recv,
            device_id={"tp": dev}, device_id_type=MESH,
        )

    def exchange(c):
        return remote(snd.at[made(c)], rcv.at[held(c)], d_ss.at[c], d_rs.at[c], sibling)

    def inward(c):
        src = snd.at[made(c)] if c in HEAD else part.at[held(c)]
        return remote(src, a_rcv.at[held(c)], a_ss.at[c], a_rs.at[c], onward)

    def inward_other(c):
        dev = onward + 1 - 2 * core
        return remote(snd.at[made(c)], h_rcv.at[held(c)], h_ss.at[c], h_rs.at[c], dev)

    def across(c):
        return remote(part.at[held(c)], b_rcv.at[held(c)], b_ss.at[c], b_rs.at[c], onward)

    def across_far(c):
        return remote(part.at[held(c)], b_rcv.at[held(c)], t_ss.at[c], b_rs.at[c], far)

    def across_back(c):
        return remote(part.at[held(c)], a_rcv.at[held(c)], a_ss.at[c], a_rs.at[c], back)

    def outward(c):
        return remote(y_ref.at[:, cols(c)], y_ref.at[:, cols(c)], f_ss.at[c], f_rs.at[c], back)

    def share(c):
        return remote(y_ref.at[:, cols(c)], y_ref.at[:, cols(c)], g_ss.at[c], g_rs.at[c], sibling)

    def term(c):
        owner, u, n, _ = pieces[c]
        wd_copy(c).wait()
        t = jnp.dot(hid[...], wd_v[:, cols(c)], preferred_element_type=F32)
        for i in range(n):
            ti = t[:, i * UNIT : (i + 1) * UNIT]
            own[u + i] = ti
            snd[u + i] = ti.astype(BF16)
        if c in HEAD:

            @pl.when(jnp.logical_and(core == owner, outer))
            def _():
                inward(c).start()

            @pl.when(jnp.logical_and(core != owner, outer))
            def _():
                inward_other(c).start()

            @pl.when(jnp.logical_and(core != owner, inner))
            def _():
                exchange(c).start()
        else:

            @pl.when(core != owner)
            def _():
                exchange(c).start()

    def outer_sum(c):
        exchange(c).wait_recv()
        part[held(c)] = (own[made(c)] + rcv[held(c)].astype(F32)).astype(BF16)
        inward(c).start()

    def inner_sum(c):
        exchange(c).wait_recv()
        inward(c).wait_recv()
        total = own[made(c)] + rcv[held(c)].astype(F32) + a_rcv[held(c)].astype(F32)
        if c in HEAD:
            inward_other(c).wait_recv()
            total = total + h_rcv[held(c)].astype(F32)
        part[held(c)] = total.astype(BF16)
        across(c).start()
        if c in TAIL:
            across_far(c).start()
            across_back(c).start()

    def store_sum(c, first):
        _, u, n, at = pieces[c]
        for i in range(n):
            y_ref[:, (u + i) * UNIT : (u + i + 1) * UNIT] = (
                first[at + i].astype(F32) + b_rcv[at + i].astype(F32)
            ).astype(BF16)

    def inner_final(c):
        across(c).wait_recv()
        store_sum(c, part)
        if c not in TAIL:
            outward(c).start()
        share(c).start()

    def outer_final(c):
        if c in TAIL:
            inward(c).wait_recv()
            across(c).wait_recv()
            store_sum(c, a_rcv)
        else:
            outward(c).wait_recv()
        share(c).start()

    @pl.when(inner)
    def _():
        pl.semaphore_wait(barrier, 5)

    @pl.when(outer)
    def _():
        pl.semaphore_wait(barrier, 4)

    ends = [u + n for _, u, n, _ in pieces]
    owned = [[c for c in range(count) if pieces[c][0] == k] for k in (0, 1)]
    out_left = [[c for c in owned[k] if c not in HEAD] for k in (0, 1)]
    in_left = [list(owned[k]) for k in (0, 1)]
    for c in range(count):
        term(c)
        for k in (0, 1):
            now_out = [d for d in out_left[k] if ends[d] + OUT_LAG <= ends[c]]
            now_in = [d for d in in_left[k] if IN_START + IN_RATE * pieces[d][1] <= ends[c]]
            out_left[k] = [d for d in out_left[k] if d not in now_out]
            in_left[k] = [d for d in in_left[k] if d not in now_in]
            if now_out:

                @pl.when(jnp.logical_and(outer, core == k))
                def _():
                    for d in now_out:
                        outer_sum(d)

            if now_in:

                @pl.when(jnp.logical_and(inner, core == k))
                def _():
                    for d in now_in:
                        inner_sum(d)

    for k in (0, 1):
        mine, theirs = owned[k], owned[1 - k]

        @pl.when(jnp.logical_and(outer, core == k))
        def _():
            for d in out_left[k]:
                outer_sum(d)
            for d in mine:
                outer_final(d)
            for d in mine:
                inward(d).wait_send()
                share(d).wait_send()
            for d in theirs:
                (inward_other(d) if d in HEAD else exchange(d)).wait_send()
                share(d).wait_recv()

        @pl.when(jnp.logical_and(inner, core == k))
        def _():
            events = [(ends[d], 0, d) for d in in_left[k]]
            events += [(ends[d] + HOP, 1, d) for d in mine]
            for _, what, d in sorted(events):
                (inner_final if what else inner_sum)(d)
            for d in mine:
                across(d).wait_send()
                if d in TAIL:
                    across_far(d).wait_send()
                    across_back(d).wait_send()
                else:
                    outward(d).wait_send()
                share(d).wait_send()
            for d in theirs:
                exchange(d).wait_send()
                share(d).wait_recv()


def solution(mesh):
    def step(x, w_gate, w_up, w_down):
        rows, depth = x.shape
        width = w_gate.shape[1]
        out = w_down.shape[1]
        pieces, units, most = layout()
        n_gu = (width // GU_COLS) * GU_PARTS
        kd = depth // GU_PARTS
        count = len(pieces)
        dma = pltpu.SemaphoreType.DMA
        return pl.pallas_call(
            kernel,
            out_shape=pltpu.VMEM((rows, out), BF16),
            in_specs=[pl.BlockSpec(memory_space=pl.ANY)] * 4,
            out_specs=pl.BlockSpec(memory_space=pltpu.VMEM),
            scratch_shapes=[
                pltpu.VMEM((rows, depth), BF16),
                pltpu.VMEM((n_gu, kd, GU_COLS), BF16),
                pltpu.VMEM((n_gu, kd, GU_COLS), BF16),
                pltpu.VMEM((width, out), BF16),
                pltpu.VMEM((rows, GU_COLS), F32),
                pltpu.VMEM((rows, GU_COLS), F32),
                pltpu.VMEM((rows, width), BF16),
                pltpu.VMEM((units, rows, UNIT), F32),
                pltpu.VMEM((units, rows, UNIT), BF16),
                pltpu.VMEM((most, rows, UNIT), BF16),
                pltpu.VMEM((most, rows, UNIT), BF16),
                pltpu.VMEM((most, rows, UNIT), BF16),
                pltpu.VMEM((most, rows, UNIT), BF16),
                pltpu.VMEM((pieces[max(HEAD)][3] + pieces[max(HEAD)][2], rows, UNIT), BF16),
                dma,
                dma((n_gu,)),
                dma((n_gu,)),
            ]
            + [dma((count,))] * 14,
            compiler_params=pltpu.CompilerParams(
                collective_id=0, has_side_effects=True, vmem_limit_bytes=60 * 1024 * 1024
            ),
        )(x, w_gate, w_up, w_down)

    return jax.shard_map(
        step,
        mesh=mesh,
        in_specs=(P("dp", None), P(None, "tp"), P(None, "tp"), P("tp", None)),
        out_specs=P("dp", None),
        check_vma=False,
    )
```

time: 104 us -> 48.9 us (0.47)
  waiting for transfers between devices: 63.1 us -> 0 us
  Pallas kernels: 0 us -> 47.7 us
  matrix products: 23.2 us -> 0 us
  between operations: 13.4 us -> 0.01 us
  local copies, waits for them, and re-layouts: 3.77 us -> 1.06 us
    psum x1 -> x0, waiting for transfers between devices: 63.1 us -> none  [step(): return lax.psum(term, 'tp')]
    pallas_call x0 -> x1, Pallas kernels: none -> 47.7 us  [step(): pl.pallas_call(kernel, out_shape=pltpu.VMEM((rows, out), BF16), in_specs=...]
    dot_general x2 -> x0, matrix products: 23.2 us -> none  [the longest x1 15.5 us: step(): jnp.dot(hidden, w_down, preferred_element_type=jnp.float32)]
    unnamed x3 -> x1, local copies, waits for them, and re-layouts: 3.77 us -> 1.06 us
  transfers between devices with their start and end apart: 1 -> 0, of which waited for: 1 -> 0; matrix products, arithmetic and copies ran while one was open for 0% -> 0% of each run, Pallas kernels for 0% -> 0%
where the time goes in v4:
time: 48.9 us; the launch traced here: 48.8 us
  Pallas kernels  47.7 us (98%)
  local copies, waits for them, and re-layouts  1.06 us (2%)
    pallas_call x1, Pallas kernels, step(): pl.pallas_call(kernel, out_shape=pltpu.VMEM((rows, out), BF16), in_specs=...  47.7 us
    unnamed x1, local copies, waits for them, and re-layouts  1.06 us

profile of v4, /device:TPU:0, one launch (start us, length us, event | category | flops | bytes accessed | tf_op | source)
XLA Modules:
  0.0 48.8 jit_solution(10084377197554732570)
XLA Ops:
  0.0 47.7 %shard_map.46 = bf16[128,5120]{1,0:T(8,128)(2,1)S(1)} custom-call(bf16[128,5120]{1,0:T(8,128)(2,1)} %x_hbm.1, bf16[5120,1536]{1,0:T(8,128)(2,1)} %wg_hbm.1, bf16[5120,1536]{1,0:T(8,128)(2,1)} %wu_hbm.1, bf16[1536,5120]{1,0:T(8,128)(2,1)} %wd_hbm.1), custom_call_target="tpu_custom_call" | custom-call | tf_op jit(solution)/shard_map/pallas_call | solution.py:313
  47.7 1.1 %copy.6 = bf16[128,5120]{1,0:T(8,128)(2,1)} copy(bf16[128,5120]{1,0:T(8,128)(2,1)S(1)} %shard_map.46) | data formatting | bytes 2621440

commit v5 on v4

--- a/solution.py
+++ b/solution.py
@@ -11,24 +11,20 @@
 GU_COLS = 256
 GU_PARTS = 4
 UNIT = 128
-PIECES = (
-    (1, 1), (0, 2), (1, 2), (0, 2), (1, 3), (0, 3), (1, 4), (0, 4),
-    (1, 4), (0, 4), (1, 4), (0, 2), (1, 2), (0, 1), (1, 1), (1, 1),
-)
+GROUPS = ((1, 1),) + ((1, 0),) * 18 + ((1, 1),)
 HEAD = (0,)
-TAIL = (15,)
+TAIL = (39,)
 OUT_LAG = 9
 IN_START, IN_RATE = 28, 3.0
 HOP = 7.0
 
 
 def layout():
-    u, local, pieces = 0, [0, 0], []
-    for owner, n in PIECES:
-        pieces.append((owner, u, n, local[owner]))
-        u += n
-        local[owner] += n
-    return pieces, u, max(local)
+    local, pieces = [0, 0], []
+    for u, owner in enumerate(o for g in GROUPS for o in g):
+        pieces.append((owner, u, 1, local[owner]))
+        local[owner] += 1
+    return pieces, len(pieces), max(local)
 
 
 def kernel(
@@ -91,8 +87,11 @@
             sem.at[i],
         )
 
-    def wd_copy(c):
-        return pltpu.make_async_copy(wd_hbm.at[:, cols(c)], wd_v.at[:, cols(c)], wd_sem.at[c])
+    starts = [sum(map(len, GROUPS[:i])) for i in range(len(GROUPS) + 1)]
+
+    def wd_copy(i):
+        block = slice(starts[i] * UNIT, starts[i + 1] * UNIT)
+        return pltpu.make_async_copy(wd_hbm.at[:, block], wd_v.at[:, block], wd_sem.at[i])
 
     x_copy = pltpu.make_async_copy(x_hbm, x_v, x_sem)
     x_copy.start()
@@ -104,8 +103,8 @@
         return c
 
     lax.fori_loop(0, n_j, start_gu, 0)
-    for c in range(count):
-        wd_copy(c).start()
+    for i in range(len(GROUPS)):
+        wd_copy(i).start()
     x_copy.wait()
 
     def gate_up(j, carry):
@@ -164,32 +163,34 @@
     def share(c):
         return remote(y_ref.at[:, cols(c)], y_ref.at[:, cols(c)], g_ss.at[c], g_rs.at[c], sibling)
 
-    def term(c):
-        owner, u, n, _ = pieces[c]
-        wd_copy(c).wait()
-        t = jnp.dot(hid[...], wd_v[:, cols(c)], preferred_element_type=F32)
-        for i in range(n):
-            ti = t[:, i * UNIT : (i + 1) * UNIT]
-            own[u + i] = ti
-            snd[u + i] = ti.astype(BF16)
-        if c in HEAD:
-
-            @pl.when(jnp.logical_and(core == owner, outer))
-            def _():
-                inward(c).start()
-
-            @pl.when(jnp.logical_and(core != owner, outer))
-            def _():
-                inward_other(c).start()
-
-            @pl.when(jnp.logical_and(core != owner, inner))
-            def _():
-                exchange(c).start()
-        else:
-
-            @pl.when(core != owner)
-            def _():
-                exchange(c).start()
+    def term(i):
+        lo, hi = starts[i], starts[i + 1]
+        wd_copy(i).wait()
+        t = jnp.dot(hid[...], wd_v[:, lo * UNIT : hi * UNIT], preferred_element_type=F32)
+        for c in range(lo, hi):
+            tc = t[:, (c - lo) * UNIT : (c - lo + 1) * UNIT]
+            own[c] = tc
+            snd[c] = tc.astype(BF16)
+        for c in range(lo, hi):
+            owner = pieces[c][0]
+            if c in HEAD:
+
+                @pl.when(jnp.logical_and(core == owner, outer))
+                def _():
+                    inward(c).start()
+
+                @pl.when(jnp.logical_and(core != owner, outer))
+                def _():
+                    inward_other(c).start()
+
+                @pl.when(jnp.logical_and(core != owner, inner))
+                def _():
+                    exchange(c).start()
+            else:
+
+                @pl.when(core != owner)
+                def _():
+                    exchange(c).start()
 
     def outer_sum(c):
         exchange(c).wait_recv()
@@ -244,11 +245,11 @@
     owned = [[c for c in range(count) if pieces[c][0] == k] for k in (0, 1)]
     out_left = [[c for c in owned[k] if c not in HEAD] for k in (0, 1)]
     in_left = [list(owned[k]) for k in (0, 1)]
-    for c in range(count):
-        term(c)
+    for i in range(len(GROUPS)):
+        term(i)
         for k in (0, 1):
-            now_out = [d for d in out_left[k] if ends[d] + OUT_LAG <= ends[c]]
-            now_in = [d for d in in_left[k] if IN_START + IN_RATE * pieces[d][1] <= ends[c]]
+            now_out = [d for d in out_left[k] if ends[d] + OUT_LAG <= starts[i + 1]]
+            now_in = [d for d in in_left[k] if IN_START + IN_RATE * d <= starts[i + 1]]
             out_left[k] = [d for d in out_left[k] if d not in now_out]
             in_left[k] = [d for d in in_left[k] if d not in now_in]
             if now_out:

time: 48.9 us -> 47.7 us (0.975)
  Pallas kernels: 47.7 us -> 46.5 us
    pallas_call x1, Pallas kernels: 47.7 us -> 46.5 us  [step(): pl.pallas_call(kernel, out_shape=pltpu.VMEM((rows, out), BF16), in_specs=...]
where the time goes in v5:
time: 47.7 us; the launch traced here: 47.6 us
  Pallas kernels  46.5 us (97%)
  local copies, waits for them, and re-layouts  1.06 us (2%)
    pallas_call x1, Pallas kernels, step(): pl.pallas_call(kernel, out_shape=pltpu.VMEM((rows, out), BF16), in_specs=...  46.5 us
    unnamed x1, local copies, waits for them, and re-layouts  1.06 us

profile of v5, /device:TPU:0, one launch (start us, length us, event | category | flops | bytes accessed | tf_op | source)
XLA Modules:
  0.0 47.6 jit_solution(16500438202311237022)
XLA Ops:
  0.0 46.5 %shard_map.46 = bf16[128,5120]{1,0:T(8,128)(2,1)S(1)} custom-call(bf16[128,5120]{1,0:T(8,128)(2,1)} %x_hbm.1, bf16[5120,1536]{1,0:T(8,128)(2,1)} %wg_hbm.1, bf16[5120,1536]{1,0:T(8,128)(2,1)} %wu_hbm.1, bf16[1536,5120]{1,0:T(8,128)(2,1)} %wd_hbm.1), custom_call_target="tpu_custom_call" | custom-call | tf_op jit(solution)/shard_map/pallas_call | solution.py:314
  46.5 1.1 %copy.6 = bf16[128,5120]{1,0:T(8,128)(2,1)} copy(bf16[128,5120]{1,0:T(8,128)(2,1)S(1)} %shard_map.46) | data formatting | bytes 2621440

commit v6 on v0

v6 whole, which is shorter than its diff:
```python
import jax
import jax.numpy as jnp
from jax import lax
from jax.experimental import pallas as pl
from jax.experimental.pallas import tpu as pltpu
from jax.sharding import PartitionSpec as P

MESH = pl.DeviceIdType.MESH
F32, BF16 = jnp.float32, jnp.bfloat16

GU_COLS = 256
GU_PARTS = 4
UNIT = 128
EDGE = 1
OUT_LAG = 5
IN_START = 14
FIN_LAG = (4, 3)


def kernel(
    x_hbm, wg_hbm, wu_hbm, wd_hbm, y_ref,
    x_v, wg_v, wu_v, wd_v, g_acc, u_acc, hid, own, snd, rcv, part, a_rcv, b_rcv, h_rcv,
    x_sem, wg_sem, wu_sem, wd_sem,
    d_ss, d_rs, a_ss, a_rs, b_ss, b_rs, f_ss, f_rs, g_ss, g_rs, h_ss, h_rs, t_ss,
):
    pairs, units = wd_v.shape[0], 2 * wd_v.shape[0]
    last = units - 1
    tp = lax.axis_index("tp")
    core = lax.rem(tp, 2)
    z = lax.div(tp, 2)
    sibling = tp + 1 - 2 * core
    inner = jnp.logical_and(z > 0, z < 3)
    outer = jnp.logical_not(inner)
    low = z < 2
    step = jnp.where(low, 2, -2)
    onward = tp + step
    back = tp - step
    far = tp + 2 * step

    kd = wg_v.shape[1]
    n_j = wg_v.shape[0] // GU_PARTS
    depth = x_v.shape[1]

    def signal(dev):
        pl.semaphore_signal(barrier, inc=1, device_id={"tp": dev}, device_id_type=MESH)

    barrier = pltpu.get_barrier_semaphore()
    signal(sibling)
    signal(onward)
    signal(far)
    signal(jnp.where(inner, back, onward) + 1 - 2 * core)

    @pl.when(inner)
    def _():
        signal(back)

    most = pairs + 2 * EDGE
    owned = jnp.where(core == 1, most, pairs - 2 * EDGE)

    def unit(i):
        edge = jnp.where(i < 2 * EDGE, i, i + units - most)
        middle = jnp.logical_and(i >= 2 * EDGE, i < most - 2 * EDGE)
        return jnp.where(
            core == 1, jnp.where(middle, 2 * (i - EDGE), edge), 2 * (i + EDGE) + 1
        )

    def mine(u):
        middle = jnp.logical_and(u >= 2 * EDGE, u < units - 2 * EDGE)
        zero = jnp.logical_and(middle, lax.rem(u, 2) == 1)
        return jnp.where(zero, 0, 1) == core

    def cols(u):
        return pl.ds(pl.multiple_of(u * UNIT, UNIT), UNIT)

    def gu_copy(hbm, vmem, sem, j, p):
        i = j * GU_PARTS + p
        return pltpu.make_async_copy(
            hbm.at[
                pl.ds(pl.multiple_of(p * kd, kd), kd),
                pl.ds(pl.multiple_of(j * GU_COLS, GU_COLS), GU_COLS),
            ],
            vmem.at[i],
            sem.at[i],
        )

    def wd_copy(k):
        block = pl.ds(pl.multiple_of(k * 2 * UNIT, 2 * UNIT), 2 * UNIT)
        return pltpu.make_async_copy(wd_hbm.at[:, block], wd_v.at[k], wd_sem.at[k])

    def loop(lo, hi, f):
        def it(k, carry):
            f(k)
            return carry

        lax.fori_loop(lo, hi, it, 0)

    x_copy = pltpu.make_async_copy(x_hbm, x_v, x_sem)
    x_copy.start()

    def start_gu(j, c):
        for p in range(GU_PARTS):
            gu_copy(wg_hbm, wg_v, wg_sem, j, p).start()
            gu_copy(wu_hbm, wu_v, wu_sem, j, p).start()
        return c

    lax.fori_loop(0, n_j, start_gu, 0)
    loop(0, pairs, lambda k: wd_copy(k).start())
    x_copy.wait()

    def gate_up(j, carry):
        for p in range(GU_PARTS):
            i = j * GU_PARTS + p
            xs = x_v[:, p * kd : (p + 1) * kd]
            gu_copy(wg_hbm, wg_v, wg_sem, j, p).wait()
            gu_copy(wu_hbm, wu_v, wu_sem, j, p).wait()
            g = jnp.dot(xs, wg_v[i], preferred_element_type=F32)
            u = jnp.dot(xs, wu_v[i], preferred_element_type=F32)
            if p == 0:
                g_acc[...] = g
                u_acc[...] = u
            elif p < GU_PARTS - 1:
                g_acc[...] += g
                u_acc[...] += u
            else:
                g = g_acc[...] + g
                u = u_acc[...] + u
                hid[:, pl.ds(pl.multiple_of(j * GU_COLS, GU_COLS), GU_COLS)] = (
                    jax.nn.silu(g) * u
                ).astype(BF16)
        return carry

    lax.fori_loop(0, n_j, gate_up, 0)

    def remote(src, dst, send, recv, dev):
        return pltpu.make_async_remote_copy(
            src_ref=src, dst_ref=dst, send_sem=send, recv_sem=recv,
            device_id={"tp": dev}, device_id_type=MESH,
        )

    def exchange(u):
        return remote(snd.at[u], rcv.at[u], d_ss.at[u], d_rs.at[u], sibling)

    def inward(u):
        return remote(part.at[u], a_rcv.at[u], a_ss.at[u], a_rs.at[u], onward)

    def head_own():
        return remote(snd.at[0], a_rcv.at[0], a_ss.at[0], a_rs.at[0], onward)

    def head_other():
        return remote(snd.at[0], h_rcv, h_ss, h_rs, onward + 1 - 2 * core)

    def across(u):
        return remote(part.at[u], b_rcv.at[u], b_ss.at[u], b_rs.at[u], onward)

    def across_far():
        return remote(part.at[last], b_rcv.at[last], t_ss, b_rs.at[last], far)

    def across_back():
        return remote(part.at[last], a_rcv.at[last], a_ss.at[last], a_rs.at[last], back)

    def outward(u):
        return remote(y_ref.at[:, cols(u)], y_ref.at[:, cols(u)], f_ss.at[u], f_rs.at[u], back)

    def share(u):
        return remote(y_ref.at[:, cols(u)], y_ref.at[:, cols(u)], g_ss.at[u], g_rs.at[u], sibling)

    def term(k):
        wd_copy(k).wait()
        t = jnp.dot(hid[...], wd_v[k], preferred_element_type=F32)
        for i in range(2):
            ti = t[:, i * UNIT : (i + 1) * UNIT]
            own[2 * k + i] = ti
            snd[2 * k + i] = ti.astype(BF16)
        for i in range(2):
            u = 2 * k + i
            direct = jnp.logical_and(u == 0, outer)

            @pl.when(jnp.logical_and(jnp.logical_not(mine(u)), jnp.logical_not(direct)))
            def _():
                exchange(u).start()

        @pl.when(jnp.logical_and(k == 0, outer))
        def _():
            @pl.when(core == 1)
            def _():
                head_own().start()

            @pl.when(core == 0)
            def _():
                head_other().start()

    def outer_sum(u):
        exchange(u).wait_recv()
        part[u] = (own[u] + rcv[u].astype(F32)).astype(BF16)
        inward(u).start()

    def outer_sums(k):
        for i in range(2):
            u = 2 * k + i

            @pl.when(jnp.logical_and(mine(u), u > 0))
            def _():
                outer_sum(u)

    def inner_sum(i):
        u = unit(i)

        @pl.when(u == 0)
        def _():
            head_other().wait_recv()
            own[0] = own[0] + h_rcv[...].astype(F32)

        exchange(u).wait_recv()
        inward(u).wait_recv()
        part[u] = (own[u] + rcv[u].astype(F32) + a_rcv[u].astype(F32)).astype(BF16)
        across(u).start()

        @pl.when(u == last)
        def _():
            across_far().start()
            across_back().start()

    def inner_final(i):
        u = unit(i)
        across(u).wait_recv()
        y_ref[:, cols(u)] = (part[u].astype(F32) + b_rcv[u].astype(F32)).astype(BF16)

        @pl.when(u < last)
        def _():
            outward(u).start()

        share(u).start()

    def outer_final(i):
        u = unit(i)
        outward(u).wait_recv()
        share(u).start()

    @pl.when(inner)
    def _():
        pl.semaphore_wait(barrier, 5)

    @pl.when(outer)
    def _():
        pl.semaphore_wait(barrier, 4)

    def terms(k):
        term(k)

        @pl.when(jnp.logical_and(outer, k >= OUT_LAG))
        def _():
            outer_sums(k - OUT_LAG)

        @pl.when(jnp.logical_and(inner, k >= IN_START))
        def _():
            inner_sum(k - IN_START)

    loop(0, pairs, terms)

    @pl.when(outer)
    def _():
        loop(pairs - OUT_LAG, pairs, outer_sums)
        loop(0, jnp.where(core == 1, owned - 1, owned), outer_final)

        @pl.when(core == 1)
        def _():
            across_back().wait_recv()
            across(last).wait_recv()
            y_ref[:, cols(last)] = (
                a_rcv[last].astype(F32) + b_rcv[last].astype(F32)
            ).astype(BF16)
            share(last).start()

        def sent(i):
            inward(unit(i)).wait_send()

        loop(0, owned, sent)

    @pl.when(inner)
    def _():
        lag = jnp.where(core == 1, FIN_LAG[1], FIN_LAG[0])
        done = pairs - IN_START
        loop(0, done - lag, inner_final)

        def both(i):
            inner_sum(i)
            inner_final(i - lag)

        loop(done, owned, both)
        loop(owned - lag, owned, inner_final)

        def sent(i):
            u = unit(i)
            across(u).wait_send()

            @pl.when(u < last)
            def _():
                outward(u).wait_send()

            @pl.when(u == last)
            def _():
                across_far().wait_send()
                across_back().wait_send()

        loop(0, owned, sent)

    def finish(u):
        @pl.when(mine(u))
        def _():
            share(u).wait_send()

        @pl.when(jnp.logical_not(mine(u)))
        def _():
            share(u).wait_recv()
            direct = jnp.logical_and(u == 0, outer)

            @pl.when(direct)
            def _():
                head_other().wait_send()

            @pl.when(jnp.logical_not(direct))
            def _():
                exchange(u).wait_send()

    loop(0, units, finish)


def solution(mesh):
    def step(x, w_gate, w_up, w_down):
        rows, depth = x.shape
        width = w_gate.shape[1]
        out = w_down.shape[1]
        units = out // UNIT
        pairs = units // 2
        n_gu = (width // GU_COLS) * GU_PARTS
        kd = depth // GU_PARTS
        dma = pltpu.SemaphoreType.DMA
        return pl.pallas_call(
            kernel,
            out_shape=pltpu.VMEM((rows, out), BF16),
            in_specs=[pl.BlockSpec(memory_space=pl.ANY)] * 4,
            out_specs=pl.BlockSpec(memory_space=pltpu.VMEM),
            scratch_shapes=[
                pltpu.VMEM((rows, depth), BF16),
                pltpu.VMEM((n_gu, kd, GU_COLS), BF16),
                pltpu.VMEM((n_gu, kd, GU_COLS), BF16),
                pltpu.VMEM((pairs, width, 2 * UNIT), BF16),
                pltpu.VMEM((rows, GU_COLS), F32),
                pltpu.VMEM((rows, GU_COLS), F32),
                pltpu.VMEM((rows, width), BF16),
                pltpu.VMEM((units, rows, UNIT), F32),
            ]
            + [pltpu.VMEM((units, rows, UNIT), BF16)] * 5
            + [pltpu.VMEM((rows, UNIT), BF16), dma, dma((n_gu,)), dma((n_gu,)), dma((pairs,))]
            + [dma((units,))] * 10
            + [dma] * 3,
            compiler_params=pltpu.CompilerParams(
                collective_id=0, has_side_effects=True, vmem_limit_bytes=60 * 1024 * 1024
            ),
        )(x, w_gate, w_up, w_down)

    return jax.shard_map(
        step,
        mesh=mesh,
        in_specs=(P("dp", None), P(None, "tp"), P(None, "tp"), P("tp", None)),
        out_specs=P("dp", None),
        check_vma=False,
    )
```

time: 104 us -> 44.2 us (0.43)
  waiting for transfers between devices: 63.1 us -> 0 us
  Pallas kernels: 0 us -> 43 us
  matrix products: 23.2 us -> 0 us
  between operations: 13.4 us -> 0.01 us
  local copies, waits for them, and re-layouts: 3.77 us -> 1.06 us
    psum x1 -> x0, waiting for transfers between devices: 63.1 us -> none  [step(): return lax.psum(term, 'tp')]
    pallas_call x0 -> x1, Pallas kernels: none -> 43 us  [step(): pl.pallas_call(kernel, out_shape=pltpu.VMEM((rows, out), BF16), in_specs=...]
    dot_general x2 -> x0, matrix products: 23.2 us -> none  [the longest x1 15.5 us: step(): jnp.dot(hidden, w_down, preferred_element_type=jnp.float32)]
    unnamed x3 -> x1, local copies, waits for them, and re-layouts: 3.77 us -> 1.06 us
  transfers between devices with their start and end apart: 1 -> 0, of which waited for: 1 -> 0; matrix products, arithmetic and copies ran while one was open for 0% -> 0% of each run, Pallas kernels for 0% -> 0%
where the time goes in v6:
time: 44.2 us; the launch traced here: 44.1 us
  Pallas kernels  43 us (97%)
  local copies, waits for them, and re-layouts  1.06 us (2%)
    pallas_call x1, Pallas kernels, step(): pl.pallas_call(kernel, out_shape=pltpu.VMEM((rows, out), BF16), in_specs=...  43 us
    unnamed x1, local copies, waits for them, and re-layouts  1.06 us

profile of v6, /device:TPU:0, one launch (start us, length us, event | category | flops | bytes accessed | tf_op | source)
XLA Modules:
  0.0 44.1 jit_solution(14080131147307634180)
XLA Ops:
  0.0 43.0 %shard_map.46 = bf16[128,5120]{1,0:T(8,128)(2,1)S(1)} custom-call(bf16[128,5120]{1,0:T(8,128)(2,1)} %x_hbm.1, bf16[5120,1536]{1,0:T(8,128)(2,1)} %wg_hbm.1, bf16[5120,1536]{1,0:T(8,128)(2,1)} %wu_hbm.1, bf16[1536,5120]{1,0:T(8,128)(2,1)} %wd_hbm.1), custom_call_target="tpu_custom_call" | custom-call | tf_op jit(solution)/shard_map/pallas_call | solution.py:338
  43.0 1.1 %copy.6 = bf16[128,5120]{1,0:T(8,128)(2,1)} copy(bf16[128,5120]{1,0:T(8,128)(2,1)S(1)} %shard_map.46) | data formatting | bytes 2621440

commit v7 on v2

--- a/solution.py
+++ b/solution.py
@@ -15,7 +15,7 @@
 Y_COLS = 256
 D2D_LAG = 4
 IN_START = 14
-FIN_LAG = 4
+FIN_LAG = 5
 
 
 def kernel(

time: 41.9 us -> 41.9 us (level)
  no operation moved by 1% of the time
where the time goes in v7:
time: 41.9 us; the launch traced here: 41.8 us
  Pallas kernels  40.7 us (97%)
  local copies, waits for them, and re-layouts  1.06 us (3%)
    pallas_call x1, Pallas kernels, step(): pl.pallas_call(kernel, out_shape=pltpu.VMEM((rows, out), BF16), in_specs=...  40.7 us
    unnamed x1, local copies, waits for them, and re-layouts  1.06 us

profile of v7, /device:TPU:0, one launch (start us, length us, event | category | flops | bytes accessed | tf_op | source)
XLA Modules:
  0.0 41.8 jit_solution(14177219566725265008)
XLA Ops:
  0.0 40.7 %shard_map.46 = bf16[128,5120]{1,0:T(8,128)(2,1)S(1)} custom-call(bf16[128,5120]{1,0:T(8,128)(2,1)} %x_hbm.1, bf16[5120,1536]{1,0:T(8,128)(2,1)} %wg_hbm.1, bf16[5120,1536]{1,0:T(8,128)(2,1)} %wu_hbm.1, bf16[1536,5120]{1,0:T(8,128)(2,1)} %wd_hbm.1), custom_call_target="tpu_custom_call" | custom-call | tf_op jit(solution)/shard_map/pallas_call | solution.py:257
  40.7 1.1 %copy.6 = bf16[128,5120]{1,0:T(8,128)(2,1)} copy(bf16[128,5120]{1,0:T(8,128)(2,1)S(1)} %shard_map.46) | data formatting | bytes 2621440

commit v8 on v6

--- a/solution.py
+++ b/solution.py
@@ -14,7 +14,7 @@
 EDGE = 1
 OUT_LAG = 5
 IN_START = 14
-FIN_LAG = (4, 3)
+FIN_LAG = (5, 4)
 
 
 def kernel(

time: 44.2 us -> 44.1 us (level)
  no operation moved by 1% of the time
where the time goes in v8:
time: 44.1 us; the launch traced here: 44 us
  Pallas kernels  42.9 us (97%)
  local copies, waits for them, and re-layouts  1.06 us (2%)
    pallas_call x1, Pallas kernels, step(): pl.pallas_call(kernel, out_shape=pltpu.VMEM((rows, out), BF16), in_specs=...  42.9 us
    unnamed x1, local copies, waits for them, and re-layouts  1.06 us

profile of v8, /device:TPU:0, one launch (start us, length us, event | category | flops | bytes accessed | tf_op | source)
XLA Modules:
  0.0 44.0 jit_solution(16365787108473839843)
XLA Ops:
  0.0 42.9 %shard_map.46 = bf16[128,5120]{1,0:T(8,128)(2,1)S(1)} custom-call(bf16[128,5120]{1,0:T(8,128)(2,1)} %x_hbm.1, bf16[5120,1536]{1,0:T(8,128)(2,1)} %wg_hbm.1, bf16[5120,1536]{1,0:T(8,128)(2,1)} %wu_hbm.1, bf16[1536,5120]{1,0:T(8,128)(2,1)} %wd_hbm.1), custom_call_target="tpu_custom_call" | custom-call | tf_op jit(solution)/shard_map/pallas_call | solution.py:338
  42.9 1.1 %copy.6 = bf16[128,5120]{1,0:T(8,128)(2,1)} copy(bf16[128,5120]{1,0:T(8,128)(2,1)S(1)} %shard_map.46) | data formatting | bytes 2621440

commit v9 on v8

--- a/solution.py
+++ b/solution.py
@@ -11,7 +11,7 @@
 GU_COLS = 256
 GU_PARTS = 4
 UNIT = 128
-EDGE = 1
+EDGE = 2
 OUT_LAG = 5
 IN_START = 14
 FIN_LAG = (5, 4)

time: 44.1 us -> 43.8 us (level)
  no operation moved by 1% of the time
where the time goes in v9:
time: 43.8 us; the launch traced here: 43.7 us
  Pallas kernels  42.6 us (97%)
  local copies, waits for them, and re-layouts  1.06 us (2%)
    pallas_call x1, Pallas kernels, step(): pl.pallas_call(kernel, out_shape=pltpu.VMEM((rows, out), BF16), in_specs=...  42.6 us
    unnamed x1, local copies, waits for them, and re-layouts  1.06 us

profile of v9, /device:TPU:0, one launch (start us, length us, event | category | flops | bytes accessed | tf_op | source)
XLA Modules:
  0.0 43.7 jit_solution(16382959099026619191)
XLA Ops:
  0.0 42.6 %shard_map.46 = bf16[128,5120]{1,0:T(8,128)(2,1)S(1)} custom-call(bf16[128,5120]{1,0:T(8,128)(2,1)} %x_hbm.1, bf16[5120,1536]{1,0:T(8,128)(2,1)} %wg_hbm.1, bf16[5120,1536]{1,0:T(8,128)(2,1)} %wu_hbm.1, bf16[1536,5120]{1,0:T(8,128)(2,1)} %wd_hbm.1), custom_call_target="tpu_custom_call" | custom-call | tf_op jit(solution)/shard_map/pallas_call | solution.py:338
  42.6 1.1 %copy.6 = bf16[128,5120]{1,0:T(8,128)(2,1)} copy(bf16[128,5120]{1,0:T(8,128)(2,1)S(1)} %shard_map.46) | data formatting | bytes 2621440

commit v10 on v9

--- a/solution.py
+++ b/solution.py
@@ -14,12 +14,13 @@
 EDGE = 2
 OUT_LAG = 5
 IN_START = 14
+TAKE_LAG = 3
 FIN_LAG = (5, 4)
 
 
 def kernel(
     x_hbm, wg_hbm, wu_hbm, wd_hbm, y_ref,
-    x_v, wg_v, wu_v, wd_v, g_acc, u_acc, hid, own, snd, rcv, part, a_rcv, b_rcv, h_rcv,
+    x_v, wg_v, wu_v, wd_v, g_acc, u_acc, hid, own, snd, rcv, part, a_rcv, b_rcv, fin, h_rcv,
     x_sem, wg_sem, wu_sem, wd_sem,
     d_ss, d_rs, a_ss, a_rs, b_ss, b_rs, f_ss, f_rs, g_ss, g_rs, h_ss, h_rs, t_ss,
 ):
@@ -57,7 +58,7 @@
     most = pairs + 2 * EDGE
     owned = jnp.where(core == 1, most, pairs - 2 * EDGE)
 
-    def unit(i):
+    def unit(i, core=core):
         edge = jnp.where(i < 2 * EDGE, i, i + units - most)
         middle = jnp.logical_and(i >= 2 * EDGE, i < most - 2 * EDGE)
         return jnp.where(
@@ -159,10 +160,10 @@
         return remote(part.at[last], a_rcv.at[last], a_ss.at[last], a_rs.at[last], back)
 
     def outward(u):
-        return remote(y_ref.at[:, cols(u)], y_ref.at[:, cols(u)], f_ss.at[u], f_rs.at[u], back)
+        return remote(fin.at[u], fin.at[u], f_ss.at[u], f_rs.at[u], back)
 
     def share(u):
-        return remote(y_ref.at[:, cols(u)], y_ref.at[:, cols(u)], g_ss.at[u], g_rs.at[u], sibling)
+        return remote(fin.at[u], fin.at[u], g_ss.at[u], g_rs.at[u], sibling)
 
     def term(k):
         wd_copy(k).wait()
@@ -223,18 +224,29 @@
     def inner_final(i):
         u = unit(i)
         across(u).wait_recv()
-        y_ref[:, cols(u)] = (part[u].astype(F32) + b_rcv[u].astype(F32)).astype(BF16)
+        fin[u] = (part[u].astype(F32) + b_rcv[u].astype(F32)).astype(BF16)
 
         @pl.when(u < last)
         def _():
             outward(u).start()
 
         share(u).start()
+        y_ref[:, cols(u)] = fin[u]
 
     def outer_final(i):
         u = unit(i)
         outward(u).wait_recv()
         share(u).start()
+        y_ref[:, cols(u)] = fin[u]
+
+    others = units - owned
+
+    def take(i):
+        @pl.when(jnp.logical_and(i >= 0, i < others))
+        def _():
+            u = unit(i, 1 - core)
+            share(u).wait_recv()
+            y_ref[:, cols(u)] = fin[u]
 
     @pl.when(inner)
     def _():
@@ -260,16 +272,23 @@
     @pl.when(outer)
     def _():
         loop(pairs - OUT_LAG, pairs, outer_sums)
-        loop(0, jnp.where(core == 1, owned - 1, owned), outer_final)
+        mids = jnp.where(core == 1, owned - 1, owned)
+
+        def ending(i):
+            outer_final(i)
+            take(i - TAKE_LAG)
+
+        loop(0, mids, ending)
 
         @pl.when(core == 1)
         def _():
             across_back().wait_recv()
             across(last).wait_recv()
-            y_ref[:, cols(last)] = (
-                a_rcv[last].astype(F32) + b_rcv[last].astype(F32)
-            ).astype(BF16)
+            fin[last] = (a_rcv[last].astype(F32) + b_rcv[last].astype(F32)).astype(BF16)
             share(last).start()
+            y_ref[:, cols(last)] = fin[last]
+
+        loop(mids - TAKE_LAG, others, take)
 
         def sent(i):
             inward(unit(i)).wait_send()
@@ -281,13 +300,20 @@
         lag = jnp.where(core == 1, FIN_LAG[1], FIN_LAG[0])
         done = pairs - IN_START
         loop(0, done - lag, inner_final)
+        loop(0, done - lag - TAKE_LAG, take)
 
         def both(i):
             inner_sum(i)
             inner_final(i - lag)
+            take(i - lag - TAKE_LAG)
+
+        def ending(i):
+            inner_final(i)
+            take(i - TAKE_LAG)
 
         loop(done, owned, both)
-        loop(owned - lag, owned, inner_final)
+        loop(owned - lag, owned, ending)
+        loop(owned - TAKE_LAG, others, take)
 
         def sent(i):
             u = unit(i)
@@ -311,7 +337,6 @@
 
         @pl.when(jnp.logical_not(mine(u)))
         def _():
-            share(u).wait_recv()
             direct = jnp.logical_and(u == 0, outer)
 
             @pl.when(direct)
@@ -350,7 +375,7 @@
                 pltpu.VMEM((rows, width), BF16),
                 pltpu.VMEM((units, rows, UNIT), F32),
             ]
-            + [pltpu.VMEM((units, rows, UNIT), BF16)] * 5
+            + [pltpu.VMEM((units, rows, UNIT), BF16)] * 6
             + [pltpu.VMEM((rows, UNIT), BF16), dma, dma((n_gu,)), dma((n_gu,)), dma((pairs,))]
             + [dma((units,))] * 10
             + [dma] * 3,

time: 43.8 us -> 46 us (1.050)
  Pallas kernels: 42.6 us -> 44.8 us
    pallas_call x1, Pallas kernels: 42.6 us -> 44.8 us  [step(): pl.pallas_call(kernel, out_shape=pltpu.VMEM((rows, out), BF16), in_specs=...]
where the time goes in v10:
time: 46 us; the launch traced here: 45.9 us
  Pallas kernels  44.8 us (97%)
  local copies, waits for them, and re-layouts  1.06 us (2%)
    pallas_call x1, Pallas kernels, step(): pl.pallas_call(kernel, out_shape=pltpu.VMEM((rows, out), BF16), in_specs=...  44.8 us
    unnamed x1, local copies, waits for them, and re-layouts  1.06 us

profile of v10, /device:TPU:0, one launch (start us, length us, event | category | flops | bytes accessed | tf_op | source)
XLA Modules:
  0.0 45.9 jit_solution(10478776258898150108)
XLA Ops:
  0.0 44.8 %shard_map.46 = bf16[128,5120]{1,0:T(8,128)(2,1)S(1)} custom-call(bf16[128,5120]{1,0:T(8,128)(2,1)} %x_hbm.1, bf16[5120,1536]{1,0:T(8,128)(2,1)} %wg_hbm.1, bf16[5120,1536]{1,0:T(8,128)(2,1)} %wu_hbm.1, bf16[1536,5120]{1,0:T(8,128)(2,1)} %wd_hbm.1), custom_call_target="tpu_custom_call" | custom-call | tf_op jit(solution)/shard_map/pallas_call | solution.py:363
  44.8 1.1 %copy.6 = bf16[128,5120]{1,0:T(8,128)(2,1)} copy(bf16[128,5120]{1,0:T(8,128)(2,1)S(1)} %shard_map.46) | data formatting | bytes 2621440

commit v11 on v7

--- a/solution.py
+++ b/solution.py
@@ -12,10 +12,10 @@
 
 GU_COLS = 256
 GU_PARTS = 4
-Y_COLS = 256
-D2D_LAG = 4
-IN_START = 14
-FIN_LAG = 5
+Y_COLS = 128
+D2D_LAG = 8
+IN_START = 28
+FIN_LAG = 8
 
 
 def kernel(

time: 41.9 us -> 46.3 us (1.11)
  Pallas kernels: 40.7 us -> 45.1 us
    pallas_call x1, Pallas kernels: 40.7 us -> 45.1 us  [step(): pl.pallas_call(kernel, out_shape=pltpu.VMEM((rows, out), BF16), in_specs=...]
where the time goes in v11:
time: 46.3 us; the launch traced here: 46.2 us
  Pallas kernels  45.1 us (97%)
  local copies, waits for them, and re-layouts  1.06 us (2%)
    pallas_call x1, Pallas kernels, step(): pl.pallas_call(kernel, out_shape=pltpu.VMEM((rows, out), BF16), in_specs=...  45.1 us
    unnamed x1, local copies, waits for them, and re-layouts  1.06 us

profile of v11, /device:TPU:0, one launch (start us, length us, event | category | flops | bytes accessed | tf_op | source)
XLA Modules:
  0.0 46.2 jit_solution(9995617186903605831)
XLA Ops:
  0.0 45.1 %shard_map.46 = bf16[128,5120]{1,0:T(8,128)(2,1)S(1)} custom-call(bf16[128,5120]{1,0:T(8,128)(2,1)} %x_hbm.1, bf16[5120,1536]{1,0:T(8,128)(2,1)} %wg_hbm.1, bf16[5120,1536]{1,0:T(8,128)(2,1)} %wu_hbm.1, bf16[1536,5120]{1,0:T(8,128)(2,1)} %wd_hbm.1), custom_call_target="tpu_custom_call" | custom-call | tf_op jit(solution)/shard_map/pallas_call | solution.py:257
  45.1 1.1 %copy.6 = bf16[128,5120]{1,0:T(8,128)(2,1)} copy(bf16[128,5120]{1,0:T(8,128)(2,1)S(1)} %shard_map.46) | data formatting | bytes 2621440

commit v12 on v7

--- a/solution.py
+++ b/solution.py
@@ -13,8 +13,8 @@
 GU_COLS = 256
 GU_PARTS = 4
 Y_COLS = 256
-D2D_LAG = 4
-IN_START = 14
+D2D_LAG = 2
+IN_START = 8
 FIN_LAG = 5
 
 
@@ -201,6 +201,10 @@
         def _():
             inner_sum(k - IN_START)
 
+        @pl.when(jnp.logical_and(inner, k >= IN_START + FIN_LAG))
+        def _():
+            inner_final(k - IN_START - FIN_LAG)
+
         return c
 
     lax.fori_loop(0, n_k, terms, 0)
@@ -221,13 +225,13 @@
     @pl.when(inner)
     def _():
         first = n_k - IN_START
-        loop(0, first - FIN_LAG, inner_final)
 
         def both(k):
             inner_sum(k)
             inner_final(k - FIN_LAG)
 
-        loop(max(first, FIN_LAG), n_k, both)
+        assert first >= FIN_LAG
+        loop(first, n_k, both)
         loop(n_k - FIN_LAG, n_k, inner_final)
 
         def sent(k):

time: 41.9 us -> 42 us (level)
  no operation moved by 1% of the time
where the time goes in v12:
time: 42 us; the launch traced here: 41.8 us
  Pallas kernels  40.8 us (97%)
  local copies, waits for them, and re-layouts  1.06 us (3%)
    pallas_call x1, Pallas kernels, step(): pl.pallas_call(kernel, out_shape=pltpu.VMEM((rows, out), BF16), in_specs=...  40.8 us
    unnamed x1, local copies, waits for them, and re-layouts  1.06 us

profile of v12, /device:TPU:0, one launch (start us, length us, event | category | flops | bytes accessed | tf_op | source)
XLA Modules:
  0.0 41.8 jit_solution(6511408653463087690)
XLA Ops:
  0.0 40.8 %shard_map.46 = bf16[128,5120]{1,0:T(8,128)(2,1)S(1)} custom-call(bf16[128,5120]{1,0:T(8,128)(2,1)} %x_hbm.1, bf16[5120,1536]{1,0:T(8,128)(2,1)} %wg_hbm.1, bf16[5120,1536]{1,0:T(8,128)(2,1)} %wu_hbm.1, bf16[1536,5120]{1,0:T(8,128)(2,1)} %wd_hbm.1), custom_call_target="tpu_custom_call" | custom-call | tf_op jit(solution)/shard_map/pallas_call | solution.py:261
  40.8 1.1 %copy.6 = bf16[128,5120]{1,0:T(8,128)(2,1)} copy(bf16[128,5120]{1,0:T(8,128)(2,1)S(1)} %shard_map.46) | data formatting | bytes 2621440

commit v13 on v12

--- a/solution.py
+++ b/solution.py
@@ -13,6 +13,7 @@
 GU_COLS = 256
 GU_PARTS = 4
 Y_COLS = 256
+WD_PIECES = 4
 D2D_LAG = 2
 IN_START = 8
 FIN_LAG = 5
@@ -37,7 +38,8 @@
     rows, half = x_v.shape[0], x_v.shape[0] // 2
     kd = wg_v.shape[1]
     n_j = wg_v.shape[0] // GU_PARTS
-    n_k = wd_v.shape[0]
+    n_k = wd_v.shape[0] * WD_PIECES
+    wd_cols = WD_PIECES * Y_COLS
     mine = pl.ds(pl.multiple_of(core * half, half), half)
     theirs = pl.ds(pl.multiple_of((1 - core) * half, half), half)
 
@@ -69,7 +71,8 @@
         )
 
     def wd_copy(k):
-        return pltpu.make_async_copy(wd_hbm.at[:, ycols(k)], wd_v.at[k], wd_sem.at[k])
+        block = pl.ds(pl.multiple_of(k * wd_cols, wd_cols), wd_cols)
+        return pltpu.make_async_copy(wd_hbm.at[:, block], wd_v.at[k], wd_sem.at[k])
 
     x_copy(mine, 0).start()
     x_copy(theirs, 1).start()
@@ -86,7 +89,7 @@
         wd_copy(k).start()
         return c
 
-    lax.fori_loop(0, n_k, start_wd, 0)
+    lax.fori_loop(0, n_k // WD_PIECES, start_wd, 0)
 
     x_copy(mine, 0).wait()
     x_copy(theirs, 1).wait()
@@ -155,8 +158,14 @@
         )
 
     def term(k):
-        wd_copy(k).wait()
-        t = jnp.dot(hid[...], wd_v[k], preferred_element_type=F32)
+        block, at = lax.div(k, WD_PIECES), lax.rem(k, WD_PIECES)
+
+        @pl.when(at == 0)
+        def _():
+            wd_copy(block).wait()
+
+        w = wd_v[block, :, pl.ds(pl.multiple_of(at * Y_COLS, Y_COLS), Y_COLS)]
+        t = jnp.dot(hid[...], w, preferred_element_type=F32)
         own[k] = t[:half]
         snd[k] = t[half:].astype(BF16)
         d2d(k).start()
@@ -267,7 +276,7 @@
                 pltpu.VMEM((rows, depth), BF16),
                 pltpu.VMEM((n_gu, kd, GU_COLS), BF16),
                 pltpu.VMEM((n_gu, kd, GU_COLS), BF16),
-                pltpu.VMEM((n_k, width, Y_COLS), BF16),
+                pltpu.VMEM((n_k // WD_PIECES, width, WD_PIECES * Y_COLS), BF16),
                 pltpu.VMEM((rows, GU_COLS), F32),
                 pltpu.VMEM((rows, GU_COLS), F32),
                 pltpu.VMEM((rows, width), BF16),

time: 42 us -> 42.6 us (1.014)
  Pallas kernels: 40.8 us -> 41.4 us
    pallas_call x1, Pallas kernels: 40.8 us -> 41.4 us  [step(): pl.pallas_call(kernel, out_shape=pltpu.VMEM((rows, out), BF16), in_specs=...]
where the time goes in v13:
time: 42.6 us; the launch traced here: 42.5 us
  Pallas kernels  41.4 us (97%)
  local copies, waits for them, and re-layouts  1.06 us (2%)
    pallas_call x1, Pallas kernels, step(): pl.pallas_call(kernel, out_shape=pltpu.VMEM((rows, out), BF16), in_specs=...  41.4 us
    unnamed x1, local copies, waits for them, and re-layouts  1.06 us

profile of v13, /device:TPU:0, one launch (start us, length us, event | category | flops | bytes accessed | tf_op | source)
XLA Modules:
  0.0 42.5 jit_solution(7298281092655245450)
XLA Ops:
  0.0 41.4 %shard_map.46 = bf16[128,5120]{1,0:T(8,128)(2,1)S(1)} custom-call(bf16[128,5120]{1,0:T(8,128)(2,1)} %x_hbm.1, bf16[5120,1536]{1,0:T(8,128)(2,1)} %wg_hbm.1, bf16[5120,1536]{1,0:T(8,128)(2,1)} %wu_hbm.1, bf16[1536,5120]{1,0:T(8,128)(2,1)} %wd_hbm.1), custom_call_target="tpu_custom_call" | custom-call | tf_op jit(solution)/shard_map/pallas_call | solution.py:270
  41.4 1.1 %copy.6 = bf16[128,5120]{1,0:T(8,128)(2,1)} copy(bf16[128,5120]{1,0:T(8,128)(2,1)S(1)} %shard_map.46) | data formatting | bytes 2621440

commit v14 on v12

v14 whole, which is shorter than its diff:
```python
import jax
import jax.numpy as jnp
from jax import lax
from jax.experimental import pallas as pl
from jax.experimental.pallas import tpu as pltpu
from jax.sharding import PartitionSpec as P

MESH = pl.DeviceIdType.MESH
F32, BF16 = jnp.float32, jnp.bfloat16

GU_COLS = 256
GU_PARTS = 4
Y_COLS = 256
ROWS = ((80, 48), (0, 80))
D2D_LAG = 2
IN_START = 8
FIN_LAG = 5


def kernel(
    x_hbm, wg_hbm, wu_hbm, wd_hbm, y_ref,
    x_v, wg_v, wu_v, wd_v, g_acc, u_acc, hid, own, snd, rcv, part, a_rcv, b_rcv,
    x_sem, wg_sem, wu_sem, wd_sem,
    d_ss, d_rs, p_ss, p_rs, f_ss, f_rs, g_ss, g_rs,
):
    tp = lax.axis_index("tp")
    core = lax.rem(tp, 2)
    z = lax.div(tp, 2)
    sibling = tp + 1 - 2 * core
    inner = jnp.logical_and(z > 0, z < 3)
    outer = jnp.logical_not(inner)
    low = z < 2
    onward = jnp.where(low, tp + 2, tp - 2)
    back = jnp.where(low, tp - 2, tp + 2)

    kd = wg_v.shape[1]
    n_j = wg_v.shape[0] // GU_PARTS
    n_k = wd_v.shape[0]
    barrier = pltpu.get_barrier_semaphore()
    pl.semaphore_signal(barrier, inc=1, device_id={"tp": sibling}, device_id_type=MESH)
    pl.semaphore_signal(barrier, inc=1, device_id={"tp": onward}, device_id_type=MESH)

    @pl.when(inner)
    def _():
        pl.semaphore_signal(barrier, inc=1, device_id={"tp": back}, device_id_type=MESH)

    def ycols(k):
        return pl.ds(pl.multiple_of(k * Y_COLS, Y_COLS), Y_COLS)

    x_copy = pltpu.make_async_copy(x_hbm, x_v, x_sem)

    def gu_copy(hbm, vmem, sem, j, p):
        i = j * GU_PARTS + p
        return pltpu.make_async_copy(
            hbm.at[
                pl.ds(pl.multiple_of(p * kd, kd), kd),
                pl.ds(pl.multiple_of(j * GU_COLS, GU_COLS), GU_COLS),
            ],
            vmem.at[i],
            sem.at[i],
        )

    def wd_copy(k):
        return pltpu.make_async_copy(wd_hbm.at[:, ycols(k)], wd_v.at[k], wd_sem.at[k])

    x_copy.start()

    def start_gu(j, c):
        for p in range(GU_PARTS):
            gu_copy(wg_hbm, wg_v, wg_sem, j, p).start()
            gu_copy(wu_hbm, wu_v, wu_sem, j, p).start()
        return c

    lax.fori_loop(0, n_j, start_gu, 0)

    def start_wd(k, c):
        wd_copy(k).start()
        return c

    lax.fori_loop(0, n_k, start_wd, 0)

    x_copy.wait()

    def gate_up(j, c):
        for p in range(GU_PARTS):
            i = j * GU_PARTS + p
            xs = x_v[:, p * kd : (p + 1) * kd]
            gu_copy(wg_hbm, wg_v, wg_sem, j, p).wait()
            gu_copy(wu_hbm, wu_v, wu_sem, j, p).wait()
            g = jnp.dot(xs, wg_v[i], preferred_element_type=F32)
            u = jnp.dot(xs, wu_v[i], preferred_element_type=F32)
            if p == 0:
                g_acc[...] = g
                u_acc[...] = u
            elif p < GU_PARTS - 1:
                g_acc[...] += g
                u_acc[...] += u
            else:
                g = g_acc[...] + g
                u = u_acc[...] + u
                hid[:, pl.ds(pl.multiple_of(j * GU_COLS, GU_COLS), GU_COLS)] = (
                    jax.nn.silu(g) * u
                ).astype(BF16)
        return c

    lax.fori_loop(0, n_j, gate_up, 0)

    @pl.when(inner)
    def _():
        pl.semaphore_wait(barrier, 3)

    @pl.when(outer)
    def _():
        pl.semaphore_wait(barrier, 2)

    def loop(lo, hi, f):
        def it(k, c):
            f(k)
            return c

        lax.fori_loop(lo, hi, it, 0)

    def remote(src, dst, send, recv, dev):
        return pltpu.make_async_remote_copy(
            src_ref=src, dst_ref=dst, send_sem=send, recv_sem=recv,
            device_id={"tp": dev}, device_id_type=MESH,
        )

    def run(me):
        lo, n = ROWS[me]
        other_lo, other_n = ROWS[1 - me]
        mine, theirs = pl.ds(lo, n), pl.ds(other_lo, other_n)
        top = pl.ds(0, n)

        def give(k):
            return remote(
                snd.at[k, theirs], rcv.at[k, pl.ds(0, other_n)], d_ss.at[k], d_rs.at[k], sibling
            )

        def got(k):
            return remote(snd.at[k, mine], rcv.at[k, top], d_ss.at[k], d_rs.at[k], sibling)

        def to_inner(k):
            return remote(
                part.at[k, top], a_rcv.at[k, top], p_ss.at[k], p_rs.at[0, k], onward
            )

        def across(k):
            return remote(
                part.at[k, top], b_rcv.at[k, top], p_ss.at[k], p_rs.at[1, k], onward
            )

        def to_outer(k):
            y_k = y_ref.at[mine, ycols(k)]
            return remote(y_k, y_k, f_ss.at[k], f_rs.at[k], back)

        def share(k):
            y_k = y_ref.at[mine, ycols(k)]
            return remote(y_k, y_k, g_ss.at[k], g_rs.at[k], sibling)

        def shared(k):
            y_k = y_ref.at[theirs, ycols(k)]
            return remote(y_k, y_k, g_ss.at[k], g_rs.at[k], sibling)

        def term(k):
            wd_copy(k).wait()
            t = jnp.dot(hid[...], wd_v[k], preferred_element_type=F32)
            own[k, top] = t[lo : lo + n]
            snd[k, theirs] = t[other_lo : other_lo + other_n].astype(BF16)
            give(k).start()

        def outer_sum(k):
            got(k).wait_recv()
            part[k, top] = (own[k, top] + rcv[k, top].astype(F32)).astype(BF16)
            to_inner(k).start()

        def inner_sum(k):
            got(k).wait_recv()
            to_inner(k).wait_recv()
            part[k, top] = (
                own[k, top] + rcv[k, top].astype(F32) + a_rcv[k, top].astype(F32)
            ).astype(BF16)
            across(k).start()

        def inner_final(k):
            across(k).wait_recv()
            y_ref[mine, ycols(k)] = (
                part[k, top].astype(F32) + b_rcv[k, top].astype(F32)
            ).astype(BF16)
            to_outer(k).start()
            share(k).start()

        def outer_final(k):
            to_outer(k).wait_recv()
            share(k).start()

        def terms(k):
            term(k)

            @pl.when(jnp.logical_and(outer, k >= D2D_LAG))
            def _():
                outer_sum(k - D2D_LAG)

            @pl.when(jnp.logical_and(inner, k >= IN_START))
            def _():
                inner_sum(k - IN_START)

            @pl.when(jnp.logical_and(inner, k >= IN_START + FIN_LAG))
            def _():
                inner_final(k - IN_START - FIN_LAG)

        loop(0, n_k, terms)

        @pl.when(outer)
        def _():
            loop(n_k - D2D_LAG, n_k, outer_sum)
            loop(0, n_k, outer_final)
            loop(0, n_k, lambda k: to_inner(k).wait_send())

        @pl.when(inner)
        def _():
            first = n_k - IN_START
            assert first >= FIN_LAG

            def both(k):
                inner_sum(k)
                inner_final(k - FIN_LAG)

            loop(first, n_k, both)
            loop(n_k - FIN_LAG, n_k, inner_final)

            def sent(k):
                across(k).wait_send()
                to_outer(k).wait_send()

            loop(0, n_k, sent)

        def finish(k):
            give(k).wait_send()
            share(k).wait_send()
            shared(k).wait_recv()

        loop(0, n_k, finish)

    for me in (0, 1):

        @pl.when(core == me)
        def _():
            run(me)


def solution(mesh):
    def step(x, w_gate, w_up, w_down):
        rows, depth = x.shape
        width = w_gate.shape[1]
        out = w_down.shape[1]
        most = max(n for _, n in ROWS)
        n_gu = (width // GU_COLS) * GU_PARTS
        n_k = out // Y_COLS
        kd = depth // GU_PARTS
        dma = pltpu.SemaphoreType.DMA
        return pl.pallas_call(
            kernel,
            out_shape=pltpu.VMEM((rows, out), BF16),
            in_specs=[pl.BlockSpec(memory_space=pl.ANY)] * 4,
            out_specs=pl.BlockSpec(memory_space=pltpu.VMEM),
            scratch_shapes=[
                pltpu.VMEM((rows, depth), BF16),
                pltpu.VMEM((n_gu, kd, GU_COLS), BF16),
                pltpu.VMEM((n_gu, kd, GU_COLS), BF16),
                pltpu.VMEM((n_k, width, Y_COLS), BF16),
                pltpu.VMEM((rows, GU_COLS), F32),
                pltpu.VMEM((rows, GU_COLS), F32),
                pltpu.VMEM((rows, width), BF16),
                pltpu.VMEM((n_k, most, Y_COLS), F32),
                pltpu.VMEM((n_k, rows, Y_COLS), BF16),
                pltpu.VMEM((n_k, most, Y_COLS), BF16),
                pltpu.VMEM((n_k, most, Y_COLS), BF16),
                pltpu.VMEM((n_k, most, Y_COLS), BF16),
                pltpu.VMEM((n_k, most, Y_COLS), BF16),
                dma,
                dma((n_gu,)),
                dma((n_gu,)),
                dma((n_k,)),
                dma((n_k,)),
                dma((n_k,)),
                dma((n_k,)),
                dma((2, n_k)),
                dma((n_k,)),
                dma((n_k,)),
                dma((n_k,)),
                dma((n_k,)),
            ],
            compiler_params=pltpu.CompilerParams(
                collective_id=0, has_side_effects=True, vmem_limit_bytes=58 * 1024 * 1024
            ),
        )(x, w_gate, w_up, w_down)

    return jax.shard_map(
        step,
        mesh=mesh,
        in_specs=(P("dp", None), P(None, "tp"), P(None, "tp"), P("tp", None)),
        out_specs=P("dp", None),
        check_vma=False,
    )
```

time: 42 us -> 41.6 us (level)
  no operation moved by 1% of the time
where the time goes in v14:
time: 41.6 us; the launch traced here: 41.5 us
  Pallas kernels  40.4 us (97%)
  local copies, waits for them, and re-layouts  1.06 us (3%)
    pallas_call x1, Pallas kernels, step(): pl.pallas_call(kernel, out_shape=pltpu.VMEM((rows, out), BF16), in_specs=...  40.4 us
    unnamed x1, local copies, waits for them, and re-layouts  1.06 us

profile of v14, /device:TPU:0, one launch (start us, length us, event | category | flops | bytes accessed | tf_op | source)
XLA Modules:
  0.0 41.5 jit_solution(3918858041262583150)
XLA Ops:
  0.0 40.4 %shard_map.46 = bf16[128,5120]{1,0:T(8,128)(2,1)S(1)} custom-call(bf16[128,5120]{1,0:T(8,128)(2,1)} %x_hbm.1, bf16[5120,1536]{1,0:T(8,128)(2,1)} %wg_hbm.1, bf16[5120,1536]{1,0:T(8,128)(2,1)} %wu_hbm.1, bf16[1536,5120]{1,0:T(8,128)(2,1)} %wd_hbm.1), custom_call_target="tpu_custom_call" | custom-call | tf_op jit(solution)/shard_map/pallas_call | solution.py:262
  40.4 1.1 %copy.6 = bf16[128,5120]{1,0:T(8,128)(2,1)} copy(bf16[128,5120]{1,0:T(8,128)(2,1)S(1)} %shard_map.46) | data formatting | bytes 2621440

commit v15 on v14

--- a/solution.py
+++ b/solution.py
@@ -14,12 +14,13 @@
 ROWS = ((80, 48), (0, 80))
 D2D_LAG = 2
 IN_START = 8
+TAKE_LAG = 8
 FIN_LAG = 5
 
 
 def kernel(
     x_hbm, wg_hbm, wu_hbm, wd_hbm, y_ref,
-    x_v, wg_v, wu_v, wd_v, g_acc, u_acc, hid, own, snd, rcv, part, a_rcv, b_rcv,
+    x_v, wg_v, wu_v, wd_v, g_acc, u_acc, hid, own, snd, rcv, part, a_rcv, b_rcv, fin, fin_other,
     x_sem, wg_sem, wu_sem, wd_sem,
     d_ss, d_rs, p_ss, p_rs, f_ss, f_rs, g_ss, g_rs,
 ):
@@ -151,16 +152,20 @@
             )
 
         def to_outer(k):
-            y_k = y_ref.at[mine, ycols(k)]
-            return remote(y_k, y_k, f_ss.at[k], f_rs.at[k], back)
+            return remote(fin.at[k, top], fin.at[k, top], f_ss.at[k], f_rs.at[k], back)
 
         def share(k):
-            y_k = y_ref.at[mine, ycols(k)]
-            return remote(y_k, y_k, g_ss.at[k], g_rs.at[k], sibling)
+            return remote(fin.at[k, top], fin_other.at[k, top], g_ss.at[k], g_rs.at[k], sibling)
 
         def shared(k):
-            y_k = y_ref.at[theirs, ycols(k)]
-            return remote(y_k, y_k, g_ss.at[k], g_rs.at[k], sibling)
+            got_k = fin_other.at[k, pl.ds(0, other_n)]
+            return remote(got_k, got_k, g_ss.at[k], g_rs.at[k], sibling)
+
+        def take(k):
+            @pl.when(k >= 0)
+            def _():
+                shared(k).wait_recv()
+                y_ref[theirs, ycols(k)] = fin_other[k, pl.ds(0, other_n)]
 
         def term(k):
             wd_copy(k).wait()
@@ -184,15 +189,17 @@
 
         def inner_final(k):
             across(k).wait_recv()
-            y_ref[mine, ycols(k)] = (
-                part[k, top].astype(F32) + b_rcv[k, top].astype(F32)
-            ).astype(BF16)
+            fin[k, top] = (part[k, top].astype(F32) + b_rcv[k, top].astype(F32)).astype(BF16)
             to_outer(k).start()
             share(k).start()
+            y_ref[mine, ycols(k)] = fin[k, top]
+            take(k - TAKE_LAG)
 
         def outer_final(k):
             to_outer(k).wait_recv()
             share(k).start()
+            y_ref[mine, ycols(k)] = fin[k, top]
+            take(k - TAKE_LAG)
 
         def terms(k):
             term(k)
@@ -238,8 +245,8 @@
         def finish(k):
             give(k).wait_send()
             share(k).wait_send()
-            shared(k).wait_recv()
-
+
+        loop(n_k - TAKE_LAG, n_k, take)
         loop(0, n_k, finish)
 
     for me in (0, 1):
@@ -278,6 +285,8 @@
                 pltpu.VMEM((n_k, most, Y_COLS), BF16),
                 pltpu.VMEM((n_k, most, Y_COLS), BF16),
                 pltpu.VMEM((n_k, most, Y_COLS), BF16),
+                pltpu.VMEM((n_k, most, Y_COLS), BF16),
+                pltpu.VMEM((n_k, most, Y_COLS), BF16),
                 dma,
                 dma((n_gu,)),
                 dma((n_gu,)),

time: 41.6 us -> 41.8 us (level)
  no operation moved by 1% of the time
where the time goes in v15:
time: 41.8 us; the launch traced here: 41.6 us
  Pallas kernels  40.6 us (97%)
  local copies, waits for them, and re-layouts  1.06 us (3%)
    pallas_call x1, Pallas kernels, step(): pl.pallas_call(kernel, out_shape=pltpu.VMEM((rows, out), BF16), in_specs=...  40.6 us
    unnamed x1, local copies, waits for them, and re-layouts  1.06 us

profile of v15, /device:TPU:0, one launch (start us, length us, event | category | flops | bytes accessed | tf_op | source)
XLA Modules:
  0.0 41.6 jit_solution(1331134635224567397)
XLA Ops:
  0.0 40.6 %shard_map.46 = bf16[128,5120]{1,0:T(8,128)(2,1)S(1)} custom-call(bf16[128,5120]{1,0:T(8,128)(2,1)} %x_hbm.1, bf16[5120,1536]{1,0:T(8,128)(2,1)} %wg_hbm.1, bf16[5120,1536]{1,0:T(8,128)(2,1)} %wu_hbm.1, bf16[1536,5120]{1,0:T(8,128)(2,1)} %wd_hbm.1), custom_call_target="tpu_custom_call" | custom-call | tf_op jit(solution)/shard_map/pallas_call | solution.py:269
  40.6 1.1 %copy.6 = bf16[128,5120]{1,0:T(8,128)(2,1)} copy(bf16[128,5120]{1,0:T(8,128)(2,1)S(1)} %shard_map.46) | data formatting | bytes 2621440

commit v16 on v14

--- a/solution.py
+++ b/solution.py
@@ -10,11 +10,11 @@
 
 GU_COLS = 256
 GU_PARTS = 4
-Y_COLS = 256
+Y_COLS = 512
 ROWS = ((80, 48), (0, 80))
-D2D_LAG = 2
-IN_START = 8
-FIN_LAG = 5
+D2D_LAG = 1
+IN_START = 5
+FIN_LAG = 3
 
 
 def kernel(

time: 41.6 us -> 42.4 us (1.019)
  Pallas kernels: 40.4 us -> 41.2 us
    pallas_call x1, Pallas kernels: 40.4 us -> 41.2 us  [step(): pl.pallas_call(kernel, out_shape=pltpu.VMEM((rows, out), BF16), in_specs=...]
where the time goes in v16:
time: 42.4 us; the launch traced here: 42.3 us
  Pallas kernels  41.2 us (97%)
  local copies, waits for them, and re-layouts  1.06 us (2%)
    pallas_call x1, Pallas kernels, step(): pl.pallas_call(kernel, out_shape=pltpu.VMEM((rows, out), BF16), in_specs=...  41.2 us
    unnamed x1, local copies, waits for them, and re-layouts  1.06 us

profile of v16, /device:TPU:0, one launch (start us, length us, event | category | flops | bytes accessed | tf_op | source)
XLA Modules:
  0.0 42.3 jit_solution(13408452520832377117)
XLA Ops:
  0.0 41.2 %shard_map.46 = bf16[128,5120]{1,0:T(8,128)(2,1)S(1)} custom-call(bf16[128,5120]{1,0:T(8,128)(2,1)} %x_hbm.1, bf16[5120,1536]{1,0:T(8,128)(2,1)} %wg_hbm.1, bf16[5120,1536]{1,0:T(8,128)(2,1)} %wu_hbm.1, bf16[1536,5120]{1,0:T(8,128)(2,1)} %wd_hbm.1), custom_call_target="tpu_custom_call" | custom-call | tf_op jit(solution)/shard_map/pallas_call | solution.py:262
  41.2 1.1 %copy.6 = bf16[128,5120]{1,0:T(8,128)(2,1)} copy(bf16[128,5120]{1,0:T(8,128)(2,1)S(1)} %shard_map.46) | data formatting | bytes 2621440

commit v17 on v14

--- a/solution.py
+++ b/solution.py
@@ -14,7 +14,7 @@
 ROWS = ((80, 48), (0, 80))
 D2D_LAG = 2
 IN_START = 8
-FIN_LAG = 5
+FIN_LAG = (4, 3)
 
 
 def kernel(
@@ -131,6 +131,7 @@
         other_lo, other_n = ROWS[1 - me]
         mine, theirs = pl.ds(lo, n), pl.ds(other_lo, other_n)
         top = pl.ds(0, n)
+        lag = FIN_LAG[me]
 
         def give(k):
             return remote(
@@ -205,9 +206,9 @@
             def _():
                 inner_sum(k - IN_START)
 
-            @pl.when(jnp.logical_and(inner, k >= IN_START + FIN_LAG))
+            @pl.when(jnp.logical_and(inner, k >= IN_START + lag))
             def _():
-                inner_final(k - IN_START - FIN_LAG)
+                inner_final(k - IN_START - lag)
 
         loop(0, n_k, terms)
 
@@ -220,14 +221,14 @@
         @pl.when(inner)
         def _():
             first = n_k - IN_START
-            assert first >= FIN_LAG
+            assert first >= lag
 
             def both(k):
                 inner_sum(k)
-                inner_final(k - FIN_LAG)
+                inner_final(k - lag)
 
             loop(first, n_k, both)
-            loop(n_k - FIN_LAG, n_k, inner_final)
+            loop(n_k - lag, n_k, inner_final)
 
             def sent(k):
                 across(k).wait_send()

time: 41.6 us -> 42.2 us (1.014)
  Pallas kernels: 40.4 us -> 41 us
    pallas_call x1, Pallas kernels: 40.4 us -> 41 us  [step(): pl.pallas_call(kernel, out_shape=pltpu.VMEM((rows, out), BF16), in_specs=...]
where the time goes in v17:
time: 42.2 us; the launch traced here: 42.1 us
  Pallas kernels  41 us (97%)
  local copies, waits for them, and re-layouts  1.06 us (3%)
    pallas_call x1, Pallas kernels, step(): pl.pallas_call(kernel, out_shape=pltpu.VMEM((rows, out), BF16), in_specs=...  41 us
    unnamed x1, local copies, waits for them, and re-layouts  1.06 us

profile of v17, /device:TPU:0, one launch (start us, length us, event | category | flops | bytes accessed | tf_op | source)
XLA Modules:
  0.0 42.1 jit_solution(12676494628334634364)
XLA Ops:
  0.0 41.0 %shard_map.46 = bf16[128,5120]{1,0:T(8,128)(2,1)S(1)} custom-call(bf16[128,5120]{1,0:T(8,128)(2,1)} %x_hbm.1, bf16[5120,1536]{1,0:T(8,128)(2,1)} %wg_hbm.1, bf16[5120,1536]{1,0:T(8,128)(2,1)} %wu_hbm.1, bf16[1536,5120]{1,0:T(8,128)(2,1)} %wd_hbm.1), custom_call_target="tpu_custom_call" | custom-call | tf_op jit(solution)/shard_map/pallas_call | solution.py:263
  41.0 1.1 %copy.6 = bf16[128,5120]{1,0:T(8,128)(2,1)} copy(bf16[128,5120]{1,0:T(8,128)(2,1)S(1)} %shard_map.46) | data formatting | bytes 2621440

commit v18 on v17

--- a/solution.py
+++ b/solution.py
@@ -14,7 +14,7 @@
 ROWS = ((80, 48), (0, 80))
 D2D_LAG = 2
 IN_START = 8
-FIN_LAG = (4, 3)
+FIN_LAG = ((4, 6), (3, 5))
 
 
 def kernel(
@@ -131,7 +131,7 @@
         other_lo, other_n = ROWS[1 - me]
         mine, theirs = pl.ds(lo, n), pl.ds(other_lo, other_n)
         top = pl.ds(0, n)
-        lag = FIN_LAG[me]
+        lag = jnp.where(low, *FIN_LAG[me])
 
         def give(k):
             return remote(
@@ -221,7 +221,7 @@
         @pl.when(inner)
         def _():
             first = n_k - IN_START
-            assert first >= lag
+            assert first >= max(FIN_LAG[me])
 
             def both(k):
                 inner_sum(k)

time: 42.2 us -> 41.6 us (0.986)
  Pallas kernels: 41 us -> 40.4 us
    pallas_call x1, Pallas kernels: 41 us -> 40.4 us  [step(): pl.pallas_call(kernel, out_shape=pltpu.VMEM((rows, out), BF16), in_specs=...]
where the time goes in v18:
time: 41.6 us; the launch traced here: 41.5 us
  Pallas kernels  40.4 us (97%)
  local copies, waits for them, and re-layouts  1.06 us (3%)
    pallas_call x1, Pallas kernels, step(): pl.pallas_call(kernel, out_shape=pltpu.VMEM((rows, out), BF16), in_specs=...  40.4 us
    unnamed x1, local copies, waits for them, and re-layouts  1.06 us

profile of v18, /device:TPU:0, one launch (start us, length us, event | category | flops | bytes accessed | tf_op | source)
XLA Modules:
  0.0 41.5 jit_solution(3419130095009114079)
XLA Ops:
  0.0 40.4 %shard_map.46 = bf16[128,5120]{1,0:T(8,128)(2,1)S(1)} custom-call(bf16[128,5120]{1,0:T(8,128)(2,1)} %x_hbm.1, bf16[5120,1536]{1,0:T(8,128)(2,1)} %wg_hbm.1, bf16[5120,1536]{1,0:T(8,128)(2,1)} %wu_hbm.1, bf16[1536,5120]{1,0:T(8,128)(2,1)} %wd_hbm.1), custom_call_target="tpu_custom_call" | custom-call | tf_op jit(solution)/shard_map/pallas_call | solution.py:263
  40.4 1.1 %copy.6 = bf16[128,5120]{1,0:T(8,128)(2,1)} copy(bf16[128,5120]{1,0:T(8,128)(2,1)S(1)} %shard_map.46) | data formatting | bytes 2621440

commit v19 on v14

--- a/solution.py
+++ b/solution.py
@@ -11,7 +11,7 @@
 GU_COLS = 256
 GU_PARTS = 4
 Y_COLS = 256
-ROWS = ((80, 48), (0, 80))
+ROWS = ((0, 80), (80, 48))
 D2D_LAG = 2
 IN_START = 8
 FIN_LAG = 5

time: 41.6 us -> 42.3 us (1.017)
  Pallas kernels: 40.4 us -> 41.1 us
    pallas_call x1, Pallas kernels: 40.4 us -> 41.1 us  [step(): pl.pallas_call(kernel, out_shape=pltpu.VMEM((rows, out), BF16), in_specs=...]
where the time goes in v19:
time: 42.3 us; the launch traced here: 42.2 us
  Pallas kernels  41.1 us (97%)
  local copies, waits for them, and re-layouts  1.06 us (3%)
    pallas_call x1, Pallas kernels, step(): pl.pallas_call(kernel, out_shape=pltpu.VMEM((rows, out), BF16), in_specs=...  41.1 us
    unnamed x1, local copies, waits for them, and re-layouts  1.06 us

profile of v19, /device:TPU:0, one launch (start us, length us, event | category | flops | bytes accessed | tf_op | source)
XLA Modules:
  0.0 42.2 jit_solution(12961221327323886936)
XLA Ops:
  0.0 41.1 %shard_map.46 = bf16[128,5120]{1,0:T(8,128)(2,1)S(1)} custom-call(bf16[128,5120]{1,0:T(8,128)(2,1)} %x_hbm.1, bf16[5120,1536]{1,0:T(8,128)(2,1)} %wg_hbm.1, bf16[5120,1536]{1,0:T(8,128)(2,1)} %wu_hbm.1, bf16[1536,5120]{1,0:T(8,128)(2,1)} %wd_hbm.1), custom_call_target="tpu_custom_call" | custom-call | tf_op jit(solution)/shard_map/pallas_call | solution.py:262
  41.1 1.1 %copy.6 = bf16[128,5120]{1,0:T(8,128)(2,1)} copy(bf16[128,5120]{1,0:T(8,128)(2,1)S(1)} %shard_map.46) | data formatting | bytes 2621440

commit v20 on v14

--- a/solution.py
+++ b/solution.py
@@ -12,6 +12,7 @@
 GU_PARTS = 4
 Y_COLS = 256
 ROWS = ((80, 48), (0, 80))
+FAR = 2
 D2D_LAG = 2
 IN_START = 8
 FIN_LAG = 5
@@ -21,7 +22,7 @@
     x_hbm, wg_hbm, wu_hbm, wd_hbm, y_ref,
     x_v, wg_v, wu_v, wd_v, g_acc, u_acc, hid, own, snd, rcv, part, a_rcv, b_rcv,
     x_sem, wg_sem, wu_sem, wd_sem,
-    d_ss, d_rs, p_ss, p_rs, f_ss, f_rs, g_ss, g_rs,
+    d_ss, d_rs, p_ss, p_rs, f_ss, f_rs, g_ss, g_rs, t_ss,
 ):
     tp = lax.axis_index("tp")
     core = lax.rem(tp, 2)
@@ -43,6 +44,13 @@
     @pl.when(inner)
     def _():
         pl.semaphore_signal(barrier, inc=1, device_id={"tp": back}, device_id_type=MESH)
+
+    far = jnp.where(low, tp + 4, tp - 4)
+    met = lax.rem(z, 2) == 0
+
+    @pl.when(met)
+    def _():
+        pl.semaphore_signal(barrier, inc=1, device_id={"tp": far}, device_id_type=MESH)
 
     def ycols(k):
         return pl.ds(pl.multiple_of(k * Y_COLS, Y_COLS), Y_COLS)
@@ -105,13 +113,11 @@
 
     lax.fori_loop(0, n_j, gate_up, 0)
 
-    @pl.when(inner)
-    def _():
-        pl.semaphore_wait(barrier, 3)
-
-    @pl.when(outer)
-    def _():
-        pl.semaphore_wait(barrier, 2)
+    for place, others in enumerate((3, 3, 4, 2)):
+
+        @pl.when(z == place)
+        def _():
+            pl.semaphore_wait(barrier, others)
 
     def loop(lo, hi, f):
         def it(k, c):
@@ -149,6 +155,12 @@
             return remote(
                 part.at[k, top], b_rcv.at[k, top], p_ss.at[k], p_rs.at[1, k], onward
             )
+
+        def straight(k):
+            return remote(part.at[k, top], b_rcv.at[k, top], t_ss.at[k], p_rs.at[1, k], far)
+
+        def half_out(k):
+            return remote(part.at[k, top], a_rcv.at[k, top], t_ss.at[k], p_rs.at[0, k], back)
 
         def to_outer(k):
             y_k = y_ref.at[mine, ycols(k)]
@@ -180,20 +192,42 @@
             part[k, top] = (
                 own[k, top] + rcv[k, top].astype(F32) + a_rcv[k, top].astype(F32)
             ).astype(BF16)
+            late = k >= n_k - FAR
+
+            @pl.when(jnp.logical_and(late, z == 2))
+            def _():
+                straight(k).start()
+
             across(k).start()
+
+            @pl.when(jnp.logical_and(late, z == 1))
+            def _():
+                half_out(k).start()
 
         def inner_final(k):
             across(k).wait_recv()
             y_ref[mine, ycols(k)] = (
                 part[k, top].astype(F32) + b_rcv[k, top].astype(F32)
             ).astype(BF16)
-            to_outer(k).start()
+
+            @pl.when(jnp.logical_or(k < n_k - FAR, z == 2))
+            def _():
+                to_outer(k).start()
+
             share(k).start()
 
         def outer_final(k):
             to_outer(k).wait_recv()
             share(k).start()
 
+        def last_final(k):
+            half_out(k).wait_recv()
+            straight(k).wait_recv()
+            y_ref[mine, ycols(k)] = (
+                a_rcv[k, top].astype(F32) + b_rcv[k, top].astype(F32)
+            ).astype(BF16)
+            share(k).start()
+
         def terms(k):
             term(k)
 
@@ -214,7 +248,9 @@
         @pl.when(outer)
         def _():
             loop(n_k - D2D_LAG, n_k, outer_sum)
-            loop(0, n_k, outer_final)
+            ends = jnp.where(z == 0, n_k - FAR, n_k)
+            loop(0, ends, outer_final)
+            loop(ends, n_k, last_final)
             loop(0, n_k, lambda k: to_inner(k).wait_send())
 
         @pl.when(inner)
@@ -231,7 +267,15 @@
 
             def sent(k):
                 across(k).wait_send()
-                to_outer(k).wait_send()
+                late = k >= n_k - FAR
+
+                @pl.when(late)
+                def _():
+                    straight(k).wait_send()
+
+                @pl.when(jnp.logical_or(jnp.logical_not(late), z == 2))
+                def _():
+                    to_outer(k).wait_send()
 
             loop(0, n_k, sent)
 
@@ -290,6 +334,7 @@
                 dma((n_k,)),
                 dma((n_k,)),
                 dma((n_k,)),
+                dma((n_k,)),
             ],
             compiler_params=pltpu.CompilerParams(
                 collective_id=0, has_side_effects=True, vmem_limit_bytes=58 * 1024 * 1024

time: 41.6 us -> 43.3 us (1.041)
  Pallas kernels: 40.4 us -> 42.1 us
    pallas_call x1, Pallas kernels: 40.4 us -> 42.1 us  [step(): pl.pallas_call(kernel, out_shape=pltpu.VMEM((rows, out), BF16), in_specs=...]
where the time goes in v20:
time: 43.3 us; the launch traced here: 43.2 us
  Pallas kernels  42.1 us (97%)
  local copies, waits for them, and re-layouts  1.06 us (2%)
    pallas_call x1, Pallas kernels, step(): pl.pallas_call(kernel, out_shape=pltpu.VMEM((rows, out), BF16), in_specs=...  42.1 us
    unnamed x1, local copies, waits for them, and re-layouts  1.06 us

profile of v20, /device:TPU:0, one launch (start us, length us, event | category | flops | bytes accessed | tf_op | source)
XLA Modules:
  0.0 43.2 jit_solution(7096025277944326852)
XLA Ops:
  0.0 42.1 %shard_map.46 = bf16[128,5120]{1,0:T(8,128)(2,1)S(1)} custom-call(bf16[128,5120]{1,0:T(8,128)(2,1)} %x_hbm.1, bf16[5120,1536]{1,0:T(8,128)(2,1)} %wg_hbm.1, bf16[5120,1536]{1,0:T(8,128)(2,1)} %wu_hbm.1, bf16[1536,5120]{1,0:T(8,128)(2,1)} %wd_hbm.1), custom_call_target="tpu_custom_call" | custom-call | tf_op jit(solution)/shard_map/pallas_call | solution.py:306
  42.1 1.1 %copy.6 = bf16[128,5120]{1,0:T(8,128)(2,1)} copy(bf16[128,5120]{1,0:T(8,128)(2,1)S(1)} %shard_map.46) | data formatting | bytes 2621440

commit v21 on v19

--- a/solution.py
+++ b/solution.py
@@ -11,7 +11,7 @@
 GU_COLS = 256
 GU_PARTS = 4
 Y_COLS = 256
-ROWS = ((0, 80), (80, 48))
+ROWS = ((72, 56), (0, 72))
 D2D_LAG = 2
 IN_START = 8
 FIN_LAG = 5

time: 42.3 us -> 41.7 us (0.986)
  Pallas kernels: 41.1 us -> 40.5 us
    pallas_call x1, Pallas kernels: 41.1 us -> 40.5 us  [step(): pl.pallas_call(kernel, out_shape=pltpu.VMEM((rows, out), BF16), in_specs=...]
where the time goes in v21:
time: 41.7 us; the launch traced here: 41.5 us
  Pallas kernels  40.5 us (97%)
  local copies, waits for them, and re-layouts  1.06 us (3%)
    pallas_call x1, Pallas kernels, step(): pl.pallas_call(kernel, out_shape=pltpu.VMEM((rows, out), BF16), in_specs=...  40.5 us
    unnamed x1, local copies, waits for them, and re-layouts  1.06 us

profile of v21, /device:TPU:0, one launch (start us, length us, event | category | flops | bytes accessed | tf_op | source)
XLA Modules:
  0.0 41.5 jit_solution(7922671004390648882)
XLA Ops:
  0.0 40.5 %shard_map.46 = bf16[128,5120]{1,0:T(8,128)(2,1)S(1)} custom-call(bf16[128,5120]{1,0:T(8,128)(2,1)} %x_hbm.1, bf16[5120,1536]{1,0:T(8,128)(2,1)} %wg_hbm.1, bf16[5120,1536]{1,0:T(8,128)(2,1)} %wu_hbm.1, bf16[1536,5120]{1,0:T(8,128)(2,1)} %wd_hbm.1), custom_call_target="tpu_custom_call" | custom-call | tf_op jit(solution)/shard_map/pallas_call | solution.py:262
  40.5 1.1 %copy.6 = bf16[128,5120]{1,0:T(8,128)(2,1)} copy(bf16[128,5120]{1,0:T(8,128)(2,1)S(1)} %shard_map.46) | data formatting | bytes 2621440

commit v22 on v14

--- a/solution.py
+++ b/solution.py
@@ -8,8 +8,8 @@
 MESH = pl.DeviceIdType.MESH
 F32, BF16 = jnp.float32, jnp.bfloat16
 
-GU_COLS = 256
-GU_PARTS = 4
+GU_COLS = 512
+GU_PARTS = 8
 Y_COLS = 256
 ROWS = ((80, 48), (0, 80))
 D2D_LAG = 2

time: 41.6 us -> 41.4 us (level)
  no operation moved by 1% of the time
where the time goes in v22:
time: 41.4 us; the launch traced here: 41.3 us
  Pallas kernels  40.2 us (97%)
  local copies, waits for them, and re-layouts  1.06 us (3%)
    pallas_call x1, Pallas kernels, step(): pl.pallas_call(kernel, out_shape=pltpu.VMEM((rows, out), BF16), in_specs=...  40.2 us
    unnamed x1, local copies, waits for them, and re-layouts  1.06 us

profile of v22, /device:TPU:0, one launch (start us, length us, event | category | flops | bytes accessed | tf_op | source)
XLA Modules:
  0.0 41.3 jit_solution(1349023515612829135)
XLA Ops:
  0.0 40.2 %shard_map.46 = bf16[128,5120]{1,0:T(8,128)(2,1)S(1)} custom-call(bf16[128,5120]{1,0:T(8,128)(2,1)} %x_hbm.1, bf16[5120,1536]{1,0:T(8,128)(2,1)} %wg_hbm.1, bf16[5120,1536]{1,0:T(8,128)(2,1)} %wu_hbm.1, bf16[1536,5120]{1,0:T(8,128)(2,1)} %wd_hbm.1), custom_call_target="tpu_custom_call" | custom-call | tf_op jit(solution)/shard_map/pallas_call | solution.py:262
  40.2 1.1 %copy.6 = bf16[128,5120]{1,0:T(8,128)(2,1)} copy(bf16[128,5120]{1,0:T(8,128)(2,1)S(1)} %shard_map.46) | data formatting | bytes 2621440

commit v23 on v22

--- a/solution.py
+++ b/solution.py
@@ -8,8 +8,8 @@
 MESH = pl.DeviceIdType.MESH
 F32, BF16 = jnp.float32, jnp.bfloat16
 
-GU_COLS = 512
-GU_PARTS = 8
+GU_COLS = 768
+GU_PARTS = 10
 Y_COLS = 256
 ROWS = ((80, 48), (0, 80))
 D2D_LAG = 2

time: 41.4 us -> 41.1 us (level)
  no operation moved by 1% of the time
where the time goes in v23:
time: 41.1 us; the launch traced here: 41 us
  Pallas kernels  39.9 us (97%)
  local copies, waits for them, and re-layouts  1.06 us (3%)
    pallas_call x1, Pallas kernels, step(): pl.pallas_call(kernel, out_shape=pltpu.VMEM((rows, out), BF16), in_specs=...  39.9 us
    unnamed x1, local copies, waits for them, and re-layouts  1.06 us

profile of v23, /device:TPU:0, one launch (start us, length us, event | category | flops | bytes accessed | tf_op | source)
XLA Modules:
  0.0 41.0 jit_solution(5285238088245767335)
XLA Ops:
  0.0 39.9 %shard_map.46 = bf16[128,5120]{1,0:T(8,128)(2,1)S(1)} custom-call(bf16[128,5120]{1,0:T(8,128)(2,1)} %x_hbm.1, bf16[5120,1536]{1,0:T(8,128)(2,1)} %wg_hbm.1, bf16[5120,1536]{1,0:T(8,128)(2,1)} %wu_hbm.1, bf16[1536,5120]{1,0:T(8,128)(2,1)} %wd_hbm.1), custom_call_target="tpu_custom_call" | custom-call | tf_op jit(solution)/shard_map/pallas_call | solution.py:262
  39.9 1.1 %copy.6 = bf16[128,5120]{1,0:T(8,128)(2,1)} copy(bf16[128,5120]{1,0:T(8,128)(2,1)S(1)} %shard_map.46) | data formatting | bytes 2621440

commit v24 on v23

--- a/solution.py
+++ b/solution.py
@@ -21,7 +21,7 @@
     x_hbm, wg_hbm, wu_hbm, wd_hbm, y_ref,
     x_v, wg_v, wu_v, wd_v, g_acc, u_acc, hid, own, snd, rcv, part, a_rcv, b_rcv,
     x_sem, wg_sem, wu_sem, wd_sem,
-    d_ss, d_rs, p_ss, p_rs, f_ss, f_rs, g_ss, g_rs,
+    d_ss, d_rs, p_ss, p_rs, f_ss, f_rs, g_ss, g_rs, t_ss,
 ):
     tp = lax.axis_index("tp")
     core = lax.rem(tp, 2)
@@ -36,9 +36,13 @@
     kd = wg_v.shape[1]
     n_j = wg_v.shape[0] // GU_PARTS
     n_k = wd_v.shape[0]
+    last = n_k - 1
     barrier = pltpu.get_barrier_semaphore()
     pl.semaphore_signal(barrier, inc=1, device_id={"tp": sibling}, device_id_type=MESH)
     pl.semaphore_signal(barrier, inc=1, device_id={"tp": onward}, device_id_type=MESH)
+
+    cross = jnp.where(inner, back, onward) + 1 - 2 * core
+    pl.semaphore_signal(barrier, inc=1, device_id={"tp": cross}, device_id_type=MESH)
 
     @pl.when(inner)
     def _():
@@ -107,11 +111,11 @@
 
     @pl.when(inner)
     def _():
-        pl.semaphore_wait(barrier, 3)
+        pl.semaphore_wait(barrier, 4)
 
     @pl.when(outer)
     def _():
-        pl.semaphore_wait(barrier, 2)
+        pl.semaphore_wait(barrier, 3)
 
     def loop(lo, hi, f):
         def it(k, c):
@@ -157,6 +161,10 @@
         def share(k):
             y_k = y_ref.at[mine, ycols(k)]
             return remote(y_k, y_k, g_ss.at[k], g_rs.at[k], sibling)
+
+        def to_other():
+            y_k = y_ref.at[mine, ycols(last)]
+            return remote(y_k, y_k, t_ss, g_rs.at[last], cross)
 
         def shared(k):
             y_k = y_ref.at[theirs, ycols(k)]
@@ -188,6 +196,11 @@
                 part[k, top].astype(F32) + b_rcv[k, top].astype(F32)
             ).astype(BF16)
             to_outer(k).start()
+
+            @pl.when(k == last)
+            def _():
+                to_other().start()
+
             share(k).start()
 
         def outer_final(k):
@@ -214,7 +227,8 @@
         @pl.when(outer)
         def _():
             loop(n_k - D2D_LAG, n_k, outer_sum)
-            loop(0, n_k, outer_final)
+            loop(0, last, outer_final)
+            to_outer(last).wait_recv()
             loop(0, n_k, lambda k: to_inner(k).wait_send())
 
         @pl.when(inner)
@@ -234,10 +248,16 @@
                 to_outer(k).wait_send()
 
             loop(0, n_k, sent)
+            to_other().wait_send()
+            share(last).wait_send()
 
         def finish(k):
             give(k).wait_send()
-            share(k).wait_send()
+
+            @pl.when(k < last)
+            def _():
+                share(k).wait_send()
+
             shared(k).wait_recv()
 
         loop(0, n_k, finish)
@@ -290,6 +310,7 @@
                 dma((n_k,)),
                 dma((n_k,)),
                 dma((n_k,)),
+                dma,
             ],
             compiler_params=pltpu.CompilerParams(
                 collective_id=0, has_side_effects=True, vmem_limit_bytes=58 * 1024 * 1024

time: 41.1 us -> 41.3 us (level)
  no operation moved by 1% of the time
where the time goes in v24:
time: 41.3 us; the launch traced here: 41.1 us
  Pallas kernels  40.1 us (97%)
  local copies, waits for them, and re-layouts  1.06 us (3%)
    pallas_call x1, Pallas kernels, step(): pl.pallas_call(kernel, out_shape=pltpu.VMEM((rows, out), BF16), in_specs=...  40.1 us
    unnamed x1, local copies, waits for them, and re-layouts  1.06 us

profile of v24, /device:TPU:0, one launch (start us, length us, event | category | flops | bytes accessed | tf_op | source)
XLA Modules:
  0.0 41.1 jit_solution(2744872290623839157)
XLA Ops:
  0.0 40.1 %shard_map.46 = bf16[128,5120]{1,0:T(8,128)(2,1)S(1)} custom-call(bf16[128,5120]{1,0:T(8,128)(2,1)} %x_hbm.1, bf16[5120,1536]{1,0:T(8,128)(2,1)} %wg_hbm.1, bf16[5120,1536]{1,0:T(8,128)(2,1)} %wu_hbm.1, bf16[1536,5120]{1,0:T(8,128)(2,1)} %wd_hbm.1), custom_call_target="tpu_custom_call" | custom-call | tf_op jit(solution)/shard_map/pallas_call | solution.py:282
  40.1 1.1 %copy.6 = bf16[128,5120]{1,0:T(8,128)(2,1)} copy(bf16[128,5120]{1,0:T(8,128)(2,1)S(1)} %shard_map.46) | data formatting | bytes 2621440

commit v25 on v23

--- a/solution.py
+++ b/solution.py
@@ -47,72 +47,6 @@
     def ycols(k):
         return pl.ds(pl.multiple_of(k * Y_COLS, Y_COLS), Y_COLS)
 
-    x_copy = pltpu.make_async_copy(x_hbm, x_v, x_sem)
-
-    def gu_copy(hbm, vmem, sem, j, p):
-        i = j * GU_PARTS + p
-        return pltpu.make_async_copy(
-            hbm.at[
-                pl.ds(pl.multiple_of(p * kd, kd), kd),
-                pl.ds(pl.multiple_of(j * GU_COLS, GU_COLS), GU_COLS),
-            ],
-            vmem.at[i],
-            sem.at[i],
-        )
-
-    def wd_copy(k):
-        return pltpu.make_async_copy(wd_hbm.at[:, ycols(k)], wd_v.at[k], wd_sem.at[k])
-
-    x_copy.start()
-
-    def start_gu(j, c):
-        for p in range(GU_PARTS):
-            gu_copy(wg_hbm, wg_v, wg_sem, j, p).start()
-            gu_copy(wu_hbm, wu_v, wu_sem, j, p).start()
-        return c
-
-    lax.fori_loop(0, n_j, start_gu, 0)
-
-    def start_wd(k, c):
-        wd_copy(k).start()
-        return c
-
-    lax.fori_loop(0, n_k, start_wd, 0)
-
-    x_copy.wait()
-
-    def gate_up(j, c):
-        for p in range(GU_PARTS):
-            i = j * GU_PARTS + p
-            xs = x_v[:, p * kd : (p + 1) * kd]
-            gu_copy(wg_hbm, wg_v, wg_sem, j, p).wait()
-            gu_copy(wu_hbm, wu_v, wu_sem, j, p).wait()
-            g = jnp.dot(xs, wg_v[i], preferred_element_type=F32)
-            u = jnp.dot(xs, wu_v[i], preferred_element_type=F32)
-            if p == 0:
-                g_acc[...] = g
-                u_acc[...] = u
-            elif p < GU_PARTS - 1:
-                g_acc[...] += g
-                u_acc[...] += u
-            else:
-                g = g_acc[...] + g
-                u = u_acc[...] + u
-                hid[:, pl.ds(pl.multiple_of(j * GU_COLS, GU_COLS), GU_COLS)] = (
-                    jax.nn.silu(g) * u
-                ).astype(BF16)
-        return c
-
-    lax.fori_loop(0, n_j, gate_up, 0)
-
-    @pl.when(inner)
-    def _():
-        pl.semaphore_wait(barrier, 3)
-
-    @pl.when(outer)
-    def _():
-        pl.semaphore_wait(barrier, 2)
-
     def loop(lo, hi, f):
         def it(k, c):
             f(k)
@@ -125,6 +59,106 @@
             src_ref=src, dst_ref=dst, send_sem=send, recv_sem=recv,
             device_id={"tp": dev}, device_id_type=MESH,
         )
+
+    depth = x_v.shape[1]
+    left, right = pl.ds(0, depth // 2), pl.ds(depth // 2, depth // 2)
+    x_left = pltpu.make_async_copy(x_hbm.at[:, left], x_v.at[:, left], x_sem.at[0])
+    x_right = pltpu.make_async_copy(x_hbm.at[:, right], x_v.at[:, right], x_sem.at[1])
+    x_gift = remote(x_v.at[:, right], x_v.at[:, right], x_sem.at[2], x_sem.at[3], sibling)
+
+    def gu_copies(hbm, vmem, sem, j, p):
+        i = j * GU_PARTS + p
+        parts = 2 if p == GU_PARTS - 1 else 1
+        n = kd // parts
+        return [
+            pltpu.make_async_copy(
+                hbm.at[
+                    pl.ds(p * kd + h * n, n),
+                    pl.ds(pl.multiple_of(j * GU_COLS, GU_COLS), GU_COLS),
+                ],
+                vmem.at[i, pl.ds(h * n, n)],
+                sem.at[j * (GU_PARTS + 1) + p + h],
+            )
+            for h in range(parts)
+        ]
+
+    def wd_copy(k):
+        return pltpu.make_async_copy(wd_hbm.at[:, ycols(k)], wd_v.at[k], wd_sem.at[k])
+
+    x_left.start()
+
+    @pl.when(core == 1)
+    def _():
+        x_right.start()
+
+
+    def start_gu(j, c):
+        for p in range(GU_PARTS):
+            gate = gu_copies(wg_hbm, wg_v, wg_sem, j, p)
+            up = gu_copies(wu_hbm, wu_v, wu_sem, j, p)
+            for g, u in zip(gate, up):
+                g.start()
+                u.start()
+        return c
+
+    lax.fori_loop(0, n_j, start_gu, 0)
+
+    def start_wd(k, c):
+        wd_copy(k).start()
+        return c
+
+    lax.fori_loop(0, n_k, start_wd, 0)
+
+    @pl.when(inner)
+    def _():
+        pl.semaphore_wait(barrier, 3)
+
+    @pl.when(outer)
+    def _():
+        pl.semaphore_wait(barrier, 2)
+
+    x_left.wait()
+
+    @pl.when(core == 1)
+    def _():
+        x_right.wait()
+        x_gift.start()
+
+
+    def gate_up(j, c):
+        for p in range(GU_PARTS):
+            i = j * GU_PARTS + p
+            if p == GU_PARTS // 2:
+
+                @pl.when(jnp.logical_and(j == 0, core == 0))
+                def _():
+                    x_gift.wait_recv()
+
+            gate = gu_copies(wg_hbm, wg_v, wg_sem, j, p)
+            up = gu_copies(wu_hbm, wu_v, wu_sem, j, p)
+            n = kd // len(gate)
+            for h in range(len(gate)):
+                gate[h].wait()
+                up[h].wait()
+                lo = h * n
+                xs = x_v[:, p * kd + lo : p * kd + lo + n]
+                g = jnp.dot(xs, wg_v[i, lo : lo + n], preferred_element_type=F32)
+                u = jnp.dot(xs, wu_v[i, lo : lo + n], preferred_element_type=F32)
+                if p == 0:
+                    g_acc[...] = g
+                    u_acc[...] = u
+                elif h == 0:
+                    g_acc[...] += g
+                    u_acc[...] += u
+                else:
+                    g = g_acc[...] + g
+                    u = u_acc[...] + u
+                    hid[:, pl.ds(pl.multiple_of(j * GU_COLS, GU_COLS), GU_COLS)] = (
+                        jax.nn.silu(g) * u
+                    ).astype(BF16)
+        return c
+
+    lax.fori_loop(0, n_j, gate_up, 0)
 
     def run(me):
         lo, n = ROWS[me]
@@ -241,6 +275,10 @@
             shared(k).wait_recv()
 
         loop(0, n_k, finish)
+
+    @pl.when(core == 1)
+    def _():
+        x_gift.wait_send()
 
     for me in (0, 1):
 
@@ -278,9 +316,9 @@
                 pltpu.VMEM((n_k, most, Y_COLS), BF16),
                 pltpu.VMEM((n_k, most, Y_COLS), BF16),
                 pltpu.VMEM((n_k, most, Y_COLS), BF16),
-                dma,
-                dma((n_gu,)),
-                dma((n_gu,)),
+                dma((4,)),
+                dma((n_gu + width // GU_COLS,)),
+                dma((n_gu + width // GU_COLS,)),
                 dma((n_k,)),
                 dma((n_k,)),
                 dma((n_k,)),

time: 41.1 us -> 40.8 us (level)
  no operation moved by 1% of the time
where the time goes in v25:
time: 40.8 us; the launch traced here: 40.7 us
  Pallas kernels  39.6 us (97%)
  local copies, waits for them, and re-layouts  1.06 us (3%)
    pallas_call x1, Pallas kernels, step(): pl.pallas_call(kernel, out_shape=pltpu.VMEM((rows, out), BF16), in_specs=...  39.6 us
    unnamed x1, local copies, waits for them, and re-layouts  1.06 us

profile of v25, /device:TPU:0, one launch (start us, length us, event | category | flops | bytes accessed | tf_op | source)
XLA Modules:
  0.0 40.7 jit_solution(13198240764151072107)
XLA Ops:
  0.0 39.6 %shard_map.46 = bf16[128,5120]{1,0:T(8,128)(2,1)S(1)} custom-call(bf16[128,5120]{1,0:T(8,128)(2,1)} %x_hbm.1, bf16[5120,1536]{1,0:T(8,128)(2,1)} %wg_hbm.1, bf16[5120,1536]{1,0:T(8,128)(2,1)} %wu_hbm.1, bf16[1536,5120]{1,0:T(8,128)(2,1)} %wd_hbm.1), custom_call_target="tpu_custom_call" | custom-call | tf_op jit(solution)/shard_map/pallas_call | solution.py:300
  39.6 1.1 %copy.6 = bf16[128,5120]{1,0:T(8,128)(2,1)} copy(bf16[128,5120]{1,0:T(8,128)(2,1)S(1)} %shard_map.46) | data formatting | bytes 2621440

commit v26 on v25

--- a/solution.py
+++ b/solution.py
@@ -9,6 +9,7 @@
 F32, BF16 = jnp.float32, jnp.bfloat16
 
 GU_COLS = 768
+X_PARTS = 3
 GU_PARTS = 10
 Y_COLS = 256
 ROWS = ((80, 48), (0, 80))
@@ -61,7 +62,8 @@
         )
 
     depth = x_v.shape[1]
-    left, right = pl.ds(0, depth // 2), pl.ds(depth // 2, depth // 2)
+    split = X_PARTS * kd
+    left, right = pl.ds(0, split), pl.ds(split, depth - split)
     x_left = pltpu.make_async_copy(x_hbm.at[:, left], x_v.at[:, left], x_sem.at[0])
     x_right = pltpu.make_async_copy(x_hbm.at[:, right], x_v.at[:, right], x_sem.at[1])
     x_gift = remote(x_v.at[:, right], x_v.at[:, right], x_sem.at[2], x_sem.at[3], sibling)
@@ -128,7 +130,7 @@
     def gate_up(j, c):
         for p in range(GU_PARTS):
             i = j * GU_PARTS + p
-            if p == GU_PARTS // 2:
+            if p == X_PARTS:
 
                 @pl.when(jnp.logical_and(j == 0, core == 0))
                 def _():

time: 40.8 us -> 40.8 us (level)
  no operation moved by 1% of the time
where the time goes in v26:
time: 40.8 us; the launch traced here: 40.6 us
  Pallas kernels  39.6 us (97%)
  local copies, waits for them, and re-layouts  1.06 us (3%)
    pallas_call x1, Pallas kernels, step(): pl.pallas_call(kernel, out_shape=pltpu.VMEM((rows, out), BF16), in_specs=...  39.6 us
    unnamed x1, local copies, waits for them, and re-layouts  1.06 us

profile of v26, /device:TPU:0, one launch (start us, length us, event | category | flops | bytes accessed | tf_op | source)
XLA Modules:
  0.0 40.6 jit_solution(17294563550329419097)
XLA Ops:
  0.0 39.6 %shard_map.46 = bf16[128,5120]{1,0:T(8,128)(2,1)S(1)} custom-call(bf16[128,5120]{1,0:T(8,128)(2,1)} %x_hbm.1, bf16[5120,1536]{1,0:T(8,128)(2,1)} %wg_hbm.1, bf16[5120,1536]{1,0:T(8,128)(2,1)} %wu_hbm.1, bf16[1536,5120]{1,0:T(8,128)(2,1)} %wd_hbm.1), custom_call_target="tpu_custom_call" | custom-call | tf_op jit(solution)/shard_map/pallas_call | solution.py:302
  39.6 1.1 %copy.6 = bf16[128,5120]{1,0:T(8,128)(2,1)} copy(bf16[128,5120]{1,0:T(8,128)(2,1)S(1)} %shard_map.46) | data formatting | bytes 2621440

commit v27 on v26

--- a/solution.py
+++ b/solution.py
@@ -9,7 +9,7 @@
 F32, BF16 = jnp.float32, jnp.bfloat16
 
 GU_COLS = 768
-X_PARTS = 3
+X_PARTS = 1
 GU_PARTS = 10
 Y_COLS = 256
 ROWS = ((80, 48), (0, 80))

time: 40.8 us -> 40.8 us (level)
  no operation moved by 1% of the time
where the time goes in v27:
time: 40.8 us; the launch traced here: 40.6 us
  Pallas kernels  39.5 us (97%)
  local copies, waits for them, and re-layouts  1.06 us (3%)
    pallas_call x1, Pallas kernels, step(): pl.pallas_call(kernel, out_shape=pltpu.VMEM((rows, out), BF16), in_specs=...  39.5 us
    unnamed x1, local copies, waits for them, and re-layouts  1.06 us

profile of v27, /device:TPU:0, one launch (start us, length us, event | category | flops | bytes accessed | tf_op | source)
XLA Modules:
  0.0 40.6 jit_solution(15711681055454883869)
XLA Ops:
  0.0 39.5 %shard_map.46 = bf16[128,5120]{1,0:T(8,128)(2,1)S(1)} custom-call(bf16[128,5120]{1,0:T(8,128)(2,1)} %x_hbm.1, bf16[5120,1536]{1,0:T(8,128)(2,1)} %wg_hbm.1, bf16[5120,1536]{1,0:T(8,128)(2,1)} %wu_hbm.1, bf16[1536,5120]{1,0:T(8,128)(2,1)} %wd_hbm.1), custom_call_target="tpu_custom_call" | custom-call | tf_op jit(solution)/shard_map/pallas_call | solution.py:302
  39.6 1.1 %copy.6 = bf16[128,5120]{1,0:T(8,128)(2,1)} copy(bf16[128,5120]{1,0:T(8,128)(2,1)S(1)} %shard_map.46) | data formatting | bytes 2621440
